TPU v7x, 32 devices: a whole 2x2x4 slice. The times are simulated.
32 devices in a mesh: dp: 8 (over y, x, core), ctx: 4 (over z).
Axes of the slice: x: 2, y: 2, z: 4, core: 2. Of those that a mesh axis runs over, the one named last changes fastest.
Arguments:
- tokens: bfloat16 [16, 2048, 768], P('dp', 'ctx'), may hold values from -6 to 6
- cotangent: bfloat16 [16, 2048, 768], P('dp', 'ctx'), may hold values from -6 to 6
- proj_weights: float32 [1, 768, 2304], P(None, ('dp', 'ctx')), may hold values from -0.21875 to 0.21875
- out_weights: float32 [1, 768, 768], P(None, ('dp', 'ctx')), may hold values from -0.875 to 0.875
- router_weights: float32 [1, 768, 8], P(None, ('dp', 'ctx')), may hold values from -0.21875 to 0.21875
- norm_gains: float32 [1, 2, 768], replicated, may hold values from 0.5 to 1.5
- bias_table: float32 [1, 32, 12], replicated, may hold values from -4 to 4
- up_weights: float32 [1, 8, 768, 3072], P(None, 'dp', None, 'ctx'), may hold values from -0.21875 to 0.21875
- down_weights: float32 [1, 8, 3072, 768], P(None, 'dp', 'ctx'), may hold values from -0.109375 to 0.109375
- doc_lengths: int32 [16, 4], P('dp'), may hold values from 1 to 1536, 2048 in all within a row
- routes: int32 [16, 2048, 2], P('dp', 'ctx'), may hold values from 0 to 7, all different within a row
Outputs:
- result: bfloat16 [16, 2048, 768], P('dp', 'ctx')
- tokens_grad: bfloat16 [16, 2048, 768], P('dp', 'ctx')
- proj_grad: float32 [1, 768, 2304], P(None, ('dp', 'ctx'))
- out_grad: float32 [1, 768, 768], P(None, ('dp', 'ctx'))
- router_grad: float32 [1, 768, 8], P(None, ('dp', 'ctx'))
- gains_grad: float32 [1, 2, 768], replicated
- table_grad: float32 [1, 32, 12], replicated
- up_grad: float32 [1, 8, 768, 3072], P(None, 'dp', None, 'ctx')
- down_grad: float32 [1, 8, 3072, 768], P(None, 'dp', 'ctx')
Inputs may be any that keep to these rules, and one draw needn't show every extreme that they name: `doc_lengths`: each row holds the lengths of its sequence's 4 documents; they sum to 2048 and the longest is 1536. `routes`: each token names 2 different experts, its first choice first.
All inputs are finite; a program needn't handle non-finite values.
Results may differ from a plain program's by a relative error of at most 0.02.
Values may be sent and summed in bfloat16 or wider, within the bound.
A program may use at most 384 MiB of HBM per device.

v0:
```python
from functools import partial

import jax
import jax.numpy as jnp
from jax import lax
from jax.sharding import PartitionSpec as P

HEADS = 12
HEAD_DIM = 64
NB = 32
WIN = 1024
TOP = 2


EPS = 1e-06
NEG = -1e30
BUCKET_EDGES = [16, 21, 27, 35, 45, 58, 76, 98, 128, 166, 215, 279, 362, 470, 609, 790]


def passed_along(block, axis, distance):
    devices = range(lax.axis_size(axis))
    route = [(i - distance, i) for i in devices if i - distance in devices]
    return lax.ppermute(block, axis, route)


def rms_norm(operand, gain_vec):
    return operand * lax.rsqrt(jnp.mean(operand * operand, axis=-1, keepdims=True) + EPS) * gain_vec


def gelu_tanh(operand):
    return jax.nn.gelu(operand, approximate=True)


def bucket_index(distance):
    edge_values = jnp.array(BUCKET_EDGES, dtype=jnp.int32)
    passed = jnp.sum((distance[..., None] >= edge_values).astype(jnp.int32), axis=-1)
    return jnp.where(distance < 16, distance, 15 + passed)


def doc_of(positions, lengths):
    bounds = jnp.cumsum(lengths)[:-1]
    return jnp.sum((positions[:, None] >= bounds[None, :]).astype(jnp.int32), axis=-1)


def gate_values(logits, route_picks):
    soft_probs = jax.nn.softmax(logits, axis=-1)
    chosen = jnp.sum(soft_probs[:, None, :] * route_picks, axis=-1)
    return chosen / jnp.sum(chosen, axis=-1, keepdims=True)


def table_parts(table):
    upper = table.astype(jnp.bfloat16)
    rest = table - upper.astype(jnp.float32)
    middle = rest.astype(jnp.bfloat16)
    lower = (rest - middle.astype(jnp.float32)).astype(jnp.bfloat16)
    return jnp.stack([upper, middle, lower])


def bias_grid(bucket_hot, table):
    return jnp.einsum(
        "qkb,pbh->hqk", bucket_hot, table_parts(table), preferred_element_type=jnp.float32
    )


def score_block(queries, key_buf, rel_bias, allowed):
    raw_scores = (
        jnp.einsum("qhd,khd->hqk", queries, key_buf, preferred_element_type=jnp.float32)
        * HEAD_DIM ** (-0.5)
        + rel_bias
    )
    return jnp.where(allowed[None], raw_scores, NEG)


def attend_forward(queries, key_buf, value_buf, rel_bias, allowed):
    masked = score_block(queries, key_buf, rel_bias, allowed)
    top_score = jnp.max(masked, axis=-1, keepdims=True)
    raised = jnp.exp(masked - top_score)
    row_total = jnp.sum(raised, axis=-1, keepdims=True)
    prob_low = (raised / row_total).astype(jnp.bfloat16)
    attended = jnp.einsum("hqk,khd->qhd", prob_low, value_buf, preferred_element_type=jnp.float32)
    return (attended, top_score + jnp.log(row_total))


def attend_backward(
    queries, key_buf, value_buf, rel_bias, allowed, log_total, grad_att, bucket_hot
):
    masked = score_block(queries, key_buf, rel_bias, allowed)
    soft_probs = jnp.exp(masked - log_total)
    prob_low = soft_probs.astype(jnp.bfloat16)
    grad_probs = jnp.einsum("qhd,khd->hqk", grad_att, value_buf, preferred_element_type=jnp.float32)
    inner_sum = jnp.sum(grad_probs * soft_probs, axis=-1, keepdims=True)
    grad_scores = (soft_probs * (grad_probs - inner_sum)).astype(jnp.bfloat16)
    score_scale = HEAD_DIM ** (-0.5)
    grad_queries = (
        jnp.einsum("hqk,khd->qhd", grad_scores, key_buf, preferred_element_type=jnp.float32)
        * score_scale
    )
    grad_keys = (
        jnp.einsum("hqk,qhd->khd", grad_scores, queries, preferred_element_type=jnp.float32)
        * score_scale
    )
    grad_values = jnp.einsum("hqk,qhd->khd", prob_low, grad_att, preferred_element_type=jnp.float32)
    table_grad = jnp.einsum(
        "hqk,qkb->bh", grad_scores, bucket_hot, preferred_element_type=jnp.float32
    )
    return (grad_queries, grad_keys, grad_values, table_grad)


def to_experts(payload):
    return lax.all_to_all(payload, "dp", split_axis=0, concat_axis=1, tiled=True)


def from_experts(payload):
    return lax.all_to_all(payload, "dp", split_axis=1, concat_axis=0, tiled=True)


def fetch_weights(proj_weights, out_weights, router_weights, up_weights, down_weights):
    proj_part = proj_weights.astype(jnp.bfloat16)
    out_part = out_weights.astype(jnp.bfloat16)
    router_part = router_weights.astype(jnp.bfloat16)
    proj_full, out_full, router_full = (
        lax.all_gather(proj_part, ("dp", "ctx"), axis=1, tiled=True),
        lax.all_gather(out_part, ("dp", "ctx"), axis=1, tiled=True),
        lax.all_gather(router_part, ("dp", "ctx"), axis=1, tiled=True),
    )
    up_full, down_full = (
        lax.all_gather(up_weights.astype(jnp.bfloat16), "ctx", axis=3, tiled=True),
        lax.all_gather(down_weights.astype(jnp.bfloat16), "ctx", axis=2, tiled=True),
    )
    return (proj_full, out_full, router_full, up_full, down_full)


def on_device(
    tokens,
    cotangent,
    proj_weights,
    out_weights,
    router_weights,
    norm_gains,
    bias_table,
    up_weights,
    down_weights,
    doc_lengths,
    routes,
):
    batches, tok_rows, model_width = tokens.shape
    layer_count = proj_weights.shape[0]
    experts = lax.axis_size("dp") * up_weights.shape[1]
    capacity = max(2, 5 * TOP * tok_rows // (4 * experts))
    hop_count = (WIN + tok_rows - 2) // tok_rows
    key_rows = (hop_count + 1) * tok_rows
    base_pos = lax.axis_index("ctx") * tok_rows
    row_ids = jnp.arange(tok_rows, dtype=jnp.int32)
    col_ids = jnp.arange(key_rows, dtype=jnp.int32)
    distance = row_ids[:, None] - col_ids[None, :] + hop_count * tok_rows
    bucket_ids = jnp.clip(bucket_index(distance), 0, NB - 1)
    bucket_hot = (bucket_ids[..., None] == jnp.arange(NB, dtype=jnp.int32)).astype(jnp.bfloat16)
    rel_biases = [bias_grid(bucket_hot, bias_table[0])]
    grad_sums = [[None] * layer_count for kind_idx in range(7)]
    outputs = []
    input_grads = []
    for micro_idx in range(batches):
        forward_set = fetch_weights(
            proj_weights, out_weights, router_weights, up_weights, down_weights
        )
        lengths_now = doc_lengths[micro_idx]
        query_pos = base_pos + row_ids
        key_pos = base_pos - hop_count * tok_rows + col_ids
        query_doc = doc_of(query_pos, lengths_now)
        key_doc = doc_of(key_pos, lengths_now)
        query_gap = query_pos[:, None] - key_pos[None, :]
        allowed = (
            (key_pos[None, :] >= 0)
            & (query_gap >= 0)
            & (query_gap < WIN)
            & (query_doc[:, None] == key_doc[None, :])
        )
        route_now = routes[micro_idx]
        expert_ids = jnp.arange(experts, dtype=jnp.int32)
        route_picks = (route_now[:, :, None] == expert_ids).astype(jnp.float32)
        order_hot = (jnp.transpose(route_now).reshape(-1)[:, None] == expert_ids[None, :]).astype(
            jnp.int32
        )
        running = jnp.cumsum(order_hot, axis=0)
        slot_pos = (jnp.sum(running * order_hot, axis=-1) - 1).reshape(TOP, tok_rows)
        slot_ids = jnp.transpose(route_now) * capacity + slot_pos
        slot_range = jnp.arange(experts * capacity, dtype=jnp.int32)
        dispatch = (
            (slot_ids[:, None, :] == slot_range[None, :, None]) & (slot_pos < capacity)[:, None, :]
        ).astype(jnp.bfloat16)
        resid = tokens[micro_idx].astype(jnp.float32)
        layer_idx = 0
        layer_proj_full, layer_out_full, layer_router_full, layer_up_full, layer_down_full = (
            forward_set
        )
        layer_gains_now = norm_gains[layer_idx]
        layer_normed_low = rms_norm(resid, layer_gains_now[0]).astype(jnp.bfloat16)
        mixed_qkv = jnp.dot(
            layer_normed_low, layer_proj_full[layer_idx], preferred_element_type=jnp.float32
        ).astype(jnp.bfloat16)
        layer_queries = mixed_qkv[:, :model_width].reshape(tok_rows, HEADS, HEAD_DIM)
        own_pair = jnp.stack(
            [mixed_qkv[:, model_width : 2 * model_width], mixed_qkv[:, 2 * model_width :]]
        )
        pieces = [own_pair]
        moving = own_pair
        for layer_hop_idx in range(hop_count):
            moving = passed_along(moving, "ctx", 1)
            pieces.append(moving)
        pair_buf = jnp.concatenate(pieces[::-1], axis=1)
        layer_key_buf = pair_buf[0].reshape(key_rows, HEADS, HEAD_DIM)
        layer_value_buf = pair_buf[1].reshape(key_rows, HEADS, HEAD_DIM)
        attended, layer_log_total = attend_forward(
            layer_queries, layer_key_buf, layer_value_buf, rel_biases[layer_idx], allowed
        )
        layer_attn_low = attended.reshape(tok_rows, model_width).astype(jnp.bfloat16)
        layer_middle = resid + jnp.dot(
            layer_attn_low, layer_out_full[layer_idx], preferred_element_type=jnp.float32
        )
        layer_two_low = rms_norm(layer_middle, layer_gains_now[1]).astype(jnp.bfloat16)
        layer_logits = jnp.dot(
            layer_two_low, layer_router_full[layer_idx], preferred_element_type=jnp.float32
        )
        layer_gate_vals = gate_values(layer_logits, route_picks)
        slot_table = jnp.sum(dispatch, axis=0)
        outgoing = (
            jnp.dot(slot_table, layer_two_low, preferred_element_type=jnp.float32)
            .astype(jnp.bfloat16)
            .reshape(experts, capacity, model_width)
        )
        layer_received = to_experts(outgoing)
        layer_pre_act = jnp.einsum(
            "end,edf->enf",
            layer_received,
            layer_up_full[layer_idx],
            preferred_element_type=jnp.float32,
        )
        layer_hidden = gelu_tanh(layer_pre_act).astype(jnp.bfloat16)
        expert_out = jnp.einsum(
            "enf,efd->end",
            layer_hidden,
            layer_down_full[layer_idx],
            preferred_element_type=jnp.float32,
        ).astype(jnp.bfloat16)
        returned = from_experts(expert_out).reshape(experts * capacity, model_width)
        layer_rows_back = jnp.einsum(
            "kst,sd->ktd", dispatch, returned, preferred_element_type=jnp.float32
        )
        layer_out = layer_middle + jnp.sum(
            jnp.transpose(layer_gate_vals)[:, :, None] * layer_rows_back, axis=0
        )
        resid, layer_keep = (
            layer_out,
            (
                resid,
                layer_normed_low,
                layer_queries,
                layer_key_buf,
                layer_value_buf,
                layer_log_total,
                layer_attn_low,
                layer_middle,
                layer_two_low,
                layer_logits,
                layer_gate_vals,
                layer_received,
                layer_pre_act,
                layer_rows_back,
            ),
        )
        saved_list = [layer_keep]
        outputs.append(resid.astype(jnp.bfloat16))
        backward_set = fetch_weights(
            proj_weights, out_weights, router_weights, up_weights, down_weights
        )
        grad_resid = cotangent[micro_idx].astype(jnp.float32)
        layer_idx = 0
        layer_layer_keep = saved_list[layer_idx]
        proj_full, out_full, router_full, up_full, down_full = backward_set
        (
            layer_resid,
            normed_low,
            queries,
            key_buf,
            value_buf,
            log_total,
            attn_low,
            middle,
            two_low,
            logits,
            gate_vals,
            received,
            pre_act,
            rows_back,
        ) = layer_layer_keep
        gains_now = norm_gains[layer_idx]
        grad_gates = jnp.transpose(jnp.sum(grad_resid[None] * rows_back, axis=-1))
        scaled = (jnp.transpose(gate_vals)[:, :, None] * grad_resid[None]).astype(jnp.bfloat16)
        grad_return = (
            jnp.einsum("kst,ktd->sd", dispatch, scaled, preferred_element_type=jnp.float32)
            .astype(jnp.bfloat16)
            .reshape(experts, capacity, model_width)
        )
        grad_expert = to_experts(grad_return)
        hidden = gelu_tanh(pre_act).astype(jnp.bfloat16)
        layer_down_grad = jnp.einsum(
            "enf,end->efd", hidden, grad_expert, preferred_element_type=jnp.float32
        )
        grad_hidden = jnp.einsum(
            "end,efd->enf", grad_expert, down_full[layer_idx], preferred_element_type=jnp.float32
        )
        gelu_pull = jax.vjp(gelu_tanh, pre_act)[1]
        grad_pre = gelu_pull(grad_hidden)[0].astype(jnp.bfloat16)
        layer_up_grad = jnp.einsum(
            "end,enf->edf", received, grad_pre, preferred_element_type=jnp.float32
        )
        grad_recv = jnp.einsum(
            "enf,edf->end", grad_pre, up_full[layer_idx], preferred_element_type=jnp.float32
        ).astype(jnp.bfloat16)
        grad_send = from_experts(grad_recv).reshape(experts * capacity, model_width)
        grad_two = jnp.einsum("kst,sd->td", dispatch, grad_send, preferred_element_type=jnp.float32)
        gate_pull = jax.vjp(partial(gate_values, route_picks=route_picks), logits)[1]
        grad_logits = gate_pull(grad_gates)[0].astype(jnp.bfloat16)
        layer_router_grad = jnp.dot(
            jnp.transpose(two_low), grad_logits, preferred_element_type=jnp.float32
        )
        grad_two = grad_two + jnp.dot(
            grad_logits, jnp.transpose(router_full[layer_idx]), preferred_element_type=jnp.float32
        )
        norm_pull_two = jax.vjp(rms_norm, middle, gains_now[1])[1]
        grad_mid_norm, gain_two_grad = norm_pull_two(grad_two)
        grad_mid = grad_resid + grad_mid_norm
        grad_branch = grad_mid.astype(jnp.bfloat16)
        layer_out_grad = jnp.dot(
            jnp.transpose(attn_low), grad_branch, preferred_element_type=jnp.float32
        )
        grad_att = (
            jnp.dot(
                grad_branch, jnp.transpose(out_full[layer_idx]), preferred_element_type=jnp.float32
            )
            .astype(jnp.bfloat16)
            .reshape(tok_rows, HEADS, HEAD_DIM)
        )
        grad_queries, grad_keys, grad_values, layer_table_grad = attend_backward(
            queries,
            key_buf,
            value_buf,
            rel_biases[layer_idx],
            allowed,
            log_total,
            grad_att,
            bucket_hot,
        )
        grad_pair = jnp.stack(
            [grad_keys.reshape(key_rows, model_width), grad_values.reshape(key_rows, model_width)]
        )
        carried = grad_pair[:, :tok_rows]
        for hop_idx in range(hop_count - 1, -1, -1):
            start_row = (hop_count - hop_idx) * tok_rows
            carried = (
                passed_along(carried.astype(jnp.bfloat16), "ctx", -1).astype(carried.dtype)
                + grad_pair[:, start_row : start_row + tok_rows]
            )
        own_grad = carried.astype(jnp.bfloat16)
        grad_mixed = jnp.concatenate(
            [
                grad_queries.reshape(tok_rows, model_width).astype(jnp.bfloat16),
                own_grad[0],
                own_grad[1],
            ],
            axis=1,
        )
        layer_proj_grad = jnp.dot(
            jnp.transpose(normed_low), grad_mixed, preferred_element_type=jnp.float32
        )
        grad_norm = jnp.dot(
            grad_mixed, jnp.transpose(proj_full[layer_idx]), preferred_element_type=jnp.float32
        )
        norm_pull_one = jax.vjp(rms_norm, layer_resid, gains_now[0])[1]
        grad_resid_norm, gain_one_grad = norm_pull_one(grad_norm)
        layer_grads = (
            layer_proj_grad,
            layer_out_grad,
            layer_router_grad,
            jnp.stack([gain_one_grad, gain_two_grad]),
            layer_table_grad,
            layer_up_grad,
            layer_down_grad,
        )
        grad_resid, layer_grads = (grad_mid + grad_resid_norm, layer_grads)
        for kind_idx in range(7):
            previous = grad_sums[kind_idx][layer_idx]
            grad_sums[kind_idx][layer_idx] = (
                layer_grads[kind_idx] if previous is None else previous + layer_grads[kind_idx]
            )
        input_grads.append(grad_resid.astype(jnp.bfloat16))
    stacked = [jnp.stack(grad_sums[kind_idx]) for kind_idx in range(7)]
    proj_total, out_total, router_total, gains_total, table_total, up_total, down_total = stacked
    proj_grad, out_grad, router_grad = (
        lax.psum_scatter(proj_total, ("dp", "ctx"), scatter_dimension=1, tiled=True),
        lax.psum_scatter(out_total, ("dp", "ctx"), scatter_dimension=1, tiled=True),
        lax.psum_scatter(router_total, ("dp", "ctx"), scatter_dimension=1, tiled=True),
    )
    up_grad, down_grad = (
        lax.psum_scatter(
            up_total.astype(jnp.bfloat16), "ctx", scatter_dimension=3, tiled=True
        ).astype(jnp.float32),
        lax.psum_scatter(
            down_total.astype(jnp.bfloat16), "ctx", scatter_dimension=2, tiled=True
        ).astype(jnp.float32),
    )
    gains_grad, table_grad = lax.psum((gains_total, table_total), ("dp", "ctx"))
    return (
        jnp.stack(outputs),
        jnp.stack(input_grads),
        proj_grad,
        out_grad,
        router_grad,
        gains_grad,
        table_grad,
        up_grad,
        down_grad,
    )


def solution(mesh):
    in_specs = (
        P("dp", "ctx", None),
        P("dp", "ctx", None),
        P(None, ("dp", "ctx"), None),
        P(None, ("dp", "ctx"), None),
        P(None, ("dp", "ctx"), None),
        P(),
        P(),
        P(None, "dp", None, "ctx"),
        P(None, "dp", "ctx", None),
        P("dp", None),
        P("dp", "ctx", None),
    )
    out_specs = (
        P("dp", "ctx", None),
        P("dp", "ctx", None),
        P(None, ("dp", "ctx"), None),
        P(None, ("dp", "ctx"), None),
        P(None, ("dp", "ctx"), None),
        P(),
        P(),
        P(None, "dp", None, "ctx"),
        P(None, "dp", "ctx", None),
    )
    return jax.shard_map(
        on_device, mesh=mesh, in_specs=in_specs, out_specs=out_specs, check_vma=False
    )
```

profile of v0, /device:TPU:0, one launch (start us, length us, event | category | flops | bytes accessed | tf_op | source)
XLA Modules:
  0.0 1533.4 jit_solution(2796947120635290170)
XLA Ops:
  29.1 74.5 %all_gather.12 = bf16[1,768,8]{2,0,1:T(2,128)(2,1)S(1)} all-gather(bf16[1,24,8]{2,0,1:T(2,128)(2,1)} %copy.161), channel_id=1, replica_groups=mesh['dp'=8,'ctx'=4] {'dp','ctx'}, dimensions={1}, use_global_device_ids=true | all-gather | bytes 12672 | tf_op jit(solution)/shard_map/all_gather | solution.py:124
  104.4 17.8 %convert_reduce_fusion = s32[512,1536]{1,0:T(8,128)S(1)} fusion(s32[512,1536]{1,0:T(8,128)S(1)} %subtract_add_fusion, s32[16]{0:T(128)} %constant.84.clone), kind=kLoop, calls=%fused_computation.5 | loop fusion | flops 36962304 | bytes 6291520 | tf_op jit(solution)/shard_map/reduce_sum | solution.py:36
  126.9 18.0 %iota_compare_fusion = pred[512,1536,32]{0,2,1:T(32,128)(4,1)} fusion(s32[512,1536]{0,1:T(8,128)S(1)} %copy.158), kind=kLoop, calls=%fused_computation | loop fusion | flops 25165824 | bytes 28311552 | tf_op jit(solution)/shard_map/eq | solution.py:157
  144.9 133.9 %copy.159 = pred[512,1536,32]{1,2,0:T(32,128)(4,1)} copy(pred[512,1536,32]{0,2,1:T(32,128)(4,1)} %iota_compare_fusion) | data formatting | bytes 50331648 | tf_op jit(solution)/shard_map/eq | solution.py:157
  278.9 27.6 %fusion.220 = f32[12,512,1536]{2,0,1:T(8,128)} fusion(pred[512,1536,32]{1,2,0:T(32,128)(4,1)} %copy.159, bf16[32,12]{0,1:T(8,128)(2,1)S(1)} %convert_reduce_fusion.4), kind=kOutput, calls=%fused_computation.320 | convolution fusion | flops 603979776 | bytes 62915328 | tf_op jit(solution)/shard_map/qkb,pbh->hqk/dot_general | solution.py:60
  321.7 27.4 %collective-permute-done.2 = bf16[2,512,768]{2,1,0:T(8,128)(2,1)} collective-permute-done((bf16[2,512,768]{2,1,0:T(8,128)(2,1)S(1)}, bf16[2,512,768]{2,1,0:T(8,128)(2,1)}, u32[]{:S(2)}, u32[]{:S(2)}) %collective-permute-start.2) | collective-permute-done | bytes 1572896 | tf_op jit(solution)/shard_map/ppermute | solution.py:23
  361.7 21.1 %collective-permute-done = bf16[2,512,768]{2,1,0:T(8,128)(2,1)} collective-permute-done((bf16[2,512,768]{2,1,0:T(8,128)(2,1)S(1)}, bf16[2,512,768]{2,1,0:T(8,128)(2,1)}, u32[]{:S(2)}, u32[]{:S(2)}) %collective-permute-start) | collective-permute-done | bytes 1572896 | tf_op jit(solution)/shard_map/ppermute | solution.py:23
  395.0 21.7 %collective-permute-done.3 = bf16[2,512,768]{2,1,0:T(8,128)(2,1)} collective-permute-done((bf16[2,512,768]{2,1,0:T(8,128)(2,1)}, bf16[2,512,768]{2,1,0:T(8,128)(2,1)}, u32[]{:S(2)}, u32[]{:S(2)}) %collective-permute-start.3) | collective-permute-done | bytes 1572896 | tf_op jit(solution)/shard_map/ppermute | solution.py:23
  431.2 13.5 collective-permute-done.1
  458.8 38.0 %fusion.239 = (f32[12,512]{1,0:T(8,128)S(1)}, f32[12,512,1536]{2,1,0:T(8,128)}) fusion(f32[12,512,1536]{2,0,1:T(8,128)} %fusion.220, bf16[512,12,64]{0,2,1:T(8,128)(2,1)} %bitcast.451, bf16[1536,12,64]{0,2,1:T(8,128)(2,1)} %bitcast.435, pred[512,1536]{1,0:T(8,128)(4,1)S(1)} %get-tuple-element.114), kind=kOutput, calls=%fused_computation.384 | convolution fusion | flops 1245702144 | bytes 79454208 | tf_op jit(solution)/shard_map/qhd,khd->hqk/dot_general | solution.py:67
  496.8 16.3 %fusion.4 = f32[12,512]{1,0:T(8,128)S(1)} fusion(f32[12,512,1536]{2,1,0:T(8,128)} %get-tuple-element.131, f32[12,512]{1,0:T(8,128)S(1)} %get-tuple-element.130), kind=kLoop, calls=%fused_computation.18 | loop fusion | flops 18868224 | bytes 37797888 | tf_op jit(solution)/shard_map/reduce_sum | solution.py:78
  513.1 14.6 fusion.164
  538.6 37.0 %fusion.241 = (f32[12,512]{1,0:T(8,128)S(1)}, f32[12,512,1536]{2,1,0:T(8,128)}) fusion(f32[12,512,1536]{2,0,1:T(8,128)} %fusion.220, bf16[512,12,64]{0,2,1:T(8,128)(2,1)} %bitcast.453, bf16[1536,12,64]{0,2,1:T(8,128)(2,1)S(1)} %bitcast.437, pred[512,1536]{1,0:T(8,128)(4,1)S(1)} %get-tuple-element.115), kind=kOutput, calls=%fused_computation.386 | convolution fusion | flops 1245702144 | bytes 79454208 | tf_op jit(solution)/shard_map/qhd,khd->hqk/dot_general | solution.py:67
  575.6 16.3 %fusion.5 = f32[12,512]{1,0:T(8,128)S(1)} fusion(f32[12,512,1536]{2,1,0:T(8,128)} %get-tuple-element.137, f32[12,512]{1,0:T(8,128)S(1)} %get-tuple-element.136), kind=kLoop, calls=%fused_computation.19 | loop fusion | flops 18868224 | bytes 37797888 | tf_op jit(solution)/shard_map/reduce_sum | solution.py:78
  592.0 15.6 %fusion.163 = bf16[12,64,512]{2,1,0:T(8,128)(2,1)S(1)} fusion(bf16[1536,12,64]{0,2,1:T(8,128)(2,1)S(1)} %bitcast.450, f32[12,512,1536]{2,1,0:T(8,128)} %get-tuple-element.137, f32[12,512]{1,0:T(8,128)S(1)} %fusion.5, f32[12,512]{1,0:T(8,128)S(1)} %get-tuple-element.136), kind=kOutput, calls=%fused_computation.227 | convolution fusion | flops 1236664320 | bytes 40943616 | tf_op jit(solution)/shard_map/hqk,khd->qhd/dot_general | solution.py:80
  620.7 12.2 fusion.54
  632.9 13.8 fusion.100
  646.8 15.0 copy.221
  662.4 12.5 reduce.11
  682.3 18.5 %fusion.22 = bf16[1280,3072]{1,0:T(8,128)(2,1)S(1)} fusion(f32[1280,3072]{1,0:T(8,128)} %fusion.54, bf16[1280,768]{1,0:T(8,128)(2,1)} %bitcast.50, bf16[1,1,3072,768]{3,2,1,0:T(8,128)(2,1)} %all-gather.11.cloned.1.call-done), kind=kOutput, calls=%fused_computation.38 | convolution fusion | flops 6118440960 | bytes 30277632 | tf_op jit(solution)/shard_map/end,efd->enf/dot_general | solution.py:309
  712.3 15.0 copy.219
  727.4 14.2 reduce.10
  747.3 14.4 fusion.233
  816.2 19.6 %all-to-all-done.2 = bf16[8,160,768]{2,1,0:T(8,128)(2,1)} async-done(((bf16[8,160,768]{2,1,0:T(8,128)(2,1)}), bf16[8,160,768]{2,1,0:T(8,128)(2,1)}, u32[]{:S(2)}, u32[]{:S(2)}) %all-to-all-start.2) | async-done | bytes 1966112 | tf_op jit(solution)/shard_map/all_to_all | solution.py:110
  840.2 12.4 fusion.52
  852.6 12.8 all-to-all-done.6
  865.4 15.3 fusion.57
  880.7 18.7 %fusion.29 = bf16[1280,3072]{1,0:T(8,128)(2,1)S(1)} fusion(f32[1280,3072]{1,0:T(8,128)} %fusion.52, bf16[1280,768]{1,0:T(8,128)(2,1)} %bitcast.68, bf16[1,1,3072,768]{3,2,1,0:T(8,128)(2,1)} %all-gather.11.cloned.1.call-done), kind=kOutput, calls=%fused_computation.45 | convolution fusion | flops 6118440960 | bytes 30277632 | tf_op jit(solution)/shard_map/end,efd->enf/dot_general | solution.py:309
  910.9 15.1 copy.218
  926.0 13.8 reduce.12
  950.3 14.0 fusion.97
  964.3 15.0 copy.220
  979.3 13.8 reduce.13
  1003.3 12.2 fusion.56
  1048.6 17.1 %fusion.8 = f32[12,64,1536]{2,1,0:T(8,128)} fusion(bf16[512,12,64]{0,2,1:T(8,128)(2,1)S(1)} %bitcast.445, f32[12,512,1536]{2,1,0:T(8,128)} %get-tuple-element.137, f32[12,512]{1,0:T(8,128)S(1)} %copy-done.52), kind=kOutput, calls=%fused_computation.26 | convolution fusion | flops 1226833920 | bytes 43278336 | tf_op jit(solution)/shard_map/hqk,qhd->khd/dot_general | solution.py:102
  1065.7 26.0 %multiply_reduce_fusion = (f32[12,512]{1,0:T(8,128)S(1)}, f32[12,512,1536]{2,1,0:T(8,128)}) fusion(f32[12,512,1536]{2,1,0:T(8,128)} %get-tuple-element.137, f32[12,512]{1,0:T(8,128)S(1)} %copy-done.52, bf16[512,12,64]{0,2,1:T(8,128)(2,1)S(1)} %bitcast.446, bf16[1536,12,64]{0,2,1:T(8,128)(2,1)} %bitcast.449), kind=kOutput, calls=%fused_computation.7 | convolution fusion | flops 1236264960 | bytes 78692352 | tf_op jit(solution)/shard_map/qhd,khd->hqk/dot_general | solution.py:90
  1092.8 31.5 %multiply_convert_fusion = bf16[12,512,1536]{2,1,0:T(8,128)(2,1)} fusion(f32[12,512,1536]{2,1,0:T(8,128)} %get-tuple-element.147, f32[12,512,1536]{2,1,0:T(8,128)} %get-tuple-element.137, f32[12,512]{1,0:T(8,128)S(1)} %get-tuple-element.146, f32[12,512]{1,0:T(8,128)S(1)} %copy-done.52), kind=kLoop, calls=%fused_computation.6 | loop fusion | flops 37748736 | bytes 94420992 | tf_op jit(solution)/shard_map/convert_element_type | solution.py:92
  1137.9 27.9 %multiply_reduce_fusion.1 = (f32[12,512]{1,0:T(8,128)S(1)}, f32[12,512,1536]{2,1,0:T(8,128)}) fusion(f32[12,512,1536]{2,1,0:T(8,128)} %get-tuple-element.131, f32[12,512]{1,0:T(8,128)S(1)} %copy-done.51, bf16[512,12,64]{0,2,1:T(8,128)(2,1)S(1)} %bitcast.443, bf16[1536,12,64]{0,2,1:T(8,128)(2,1)S(1)} %bitcast.448), kind=kOutput, calls=%fused_computation.10 | convolution fusion | flops 1236264960 | bytes 78692352 | tf_op jit(solution)/shard_map/qhd,khd->hqk/dot_general | solution.py:90
  1165.8 31.3 %multiply_convert_fusion.1 = bf16[12,512,1536]{2,1,0:T(8,128)(2,1)} fusion(f32[12,512,1536]{2,1,0:T(8,128)} %get-tuple-element.145, f32[12,512,1536]{2,1,0:T(8,128)} %get-tuple-element.131, f32[12,512]{1,0:T(8,128)S(1)} %get-tuple-element.144, f32[12,512]{1,0:T(8,128)S(1)} %copy-done.51), kind=kLoop, calls=%fused_computation.9 | loop fusion | flops 37748736 | bytes 94420992 | tf_op jit(solution)/shard_map/convert_element_type | solution.py:92
  1208.9 17.0 %fusion.10 = f32[12,64,1536]{2,1,0:T(8,128)} fusion(bf16[512,12,64]{0,2,1:T(8,128)(2,1)S(1)} %bitcast.444, f32[12,512,1536]{2,1,0:T(8,128)} %get-tuple-element.131, f32[12,512]{1,0:T(8,128)S(1)} %copy-done.51), kind=kOutput, calls=%fused_computation.27 | convolution fusion | flops 1226833920 | bytes 43278336 | tf_op jit(solution)/shard_map/hqk,qhd->khd/dot_general | solution.py:102
  1249.1 21.0 %collective-permute-done.4 = bf16[2,512,768]{1,2,0:T(8,128)(2,1)} collective-permute-done((bf16[2,512,768]{1,2,0:T(8,128)(2,1)}, bf16[2,512,768]{1,2,0:T(8,128)(2,1)}, u32[]{:S(2)}, u32[]{:S(2)}) %collective-permute-start.4) | collective-permute-done | bytes 1572896 | tf_op jit(solution)/shard_map/ppermute | solution.py:23
  1286.9 23.1 %collective-permute-done.7 = bf16[2,512,768]{1,2,0:T(8,128)(2,1)} collective-permute-done((bf16[2,512,768]{1,2,0:T(8,128)(2,1)}, bf16[2,512,768]{1,2,0:T(8,128)(2,1)}, u32[]{:S(2)}, u32[]{:S(2)}) %collective-permute-start.7) | collective-permute-done | bytes 1572896 | tf_op jit(solution)/shard_map/ppermute | solution.py:23
  1312.7 34.6 %collective-permute-done.5 = bf16[2,512,768]{1,2,0:T(8,128)(2,1)} collective-permute-done((bf16[2,512,768]{1,2,0:T(8,128)(2,1)}, bf16[2,512,768]{1,2,0:T(8,128)(2,1)}, u32[]{:S(2)}, u32[]{:S(2)}) %collective-permute-start.5) | collective-permute-done | bytes 1572896 | tf_op jit(solution)/shard_map/ppermute | solution.py:23
  1360.8 31.7 %copy.176 = bf16[12,512,1536]{1,0,2:T(8,128)(2,1)} copy(bf16[12,512,1536]{2,1,0:T(8,128)(2,1)} %multiply_convert_fusion) | data formatting | bytes 37748736 | tf_op jit(solution)/shard_map/convert_element_type | solution.py:92
  1392.5 31.6 %copy.175 = bf16[12,512,1536]{1,0,2:T(8,128)(2,1)} copy(bf16[12,512,1536]{2,1,0:T(8,128)(2,1)} %multiply_convert_fusion.1) | data formatting | bytes 37748736 | tf_op jit(solution)/shard_map/convert_element_type | solution.py:92
  1426.5 18.3 %fusion.172 = f32[32,12]{0,1:T(8,128)S(1)} fusion(bf16[12,512,1536]{1,0,2:T(8,128)(2,1)} %copy.175, s32[512,1536]{0,1:T(8,128)S(1)} %copy-done.15), kind=kOutput, calls=%fused_computation.237 | convolution fusion | flops 629145600 | bytes 22021632 | tf_op jit(solution)/shard_map/hqk,qkb->bh/dot_general | solution.py:103
  1444.8 19.1 %fusion.175 = f32[1,32,12]{1,2,0:T(8,128)S(1)} fusion(f32[32,12]{0,1:T(8,128)S(1)} %fusion.172, bf16[12,512,1536]{1,0,2:T(8,128)(2,1)} %copy.176, s32[512,1536]{0,1:T(8,128)S(1)} %copy-done.15), kind=kOutput, calls=%fused_computation.240 | convolution fusion | flops 629145984 | bytes 22023168 | tf_op jit(solution)/shard_map/hqk,qkb->bh/dot_general | solution.py:103
  1472.4 42.4 %all-reduce.1 = (f32[1,768,8]{1,2,0:T(8,128)S(1)}, f32[1,2,768]{2,1,0:T(2,128)}, f32[1,32,12]{1,2,0:T(8,128)S(1)}) all-reduce(f32[1,768,8]{1,2,0:T(8,128)S(1)} %fusion.171, f32[1,2,768]{2,1,0:T(2,128)S(1)} %maximum_add_fusion, f32[1,32,12]{1,2,0:T(8,128)S(1)} %fusion.175), channel_id=4, replica_groups=mesh['dp'=8,'ctx'=4] {'dp','ctx'}, use_global_device_ids=true, to_apply=%region_50.51.clone | all-reduce | flops 8064 | bytes 64512
  (482 shorter events, 373.0 us)
Async XLA Ops:
  7.2 299.5 %all-gather.5.cloned.1.call-start = ((), (), s32[]{:S(2)}) async-start(), calls=%async_computation.12 | async-start | bytes 3649536 | tf_op jit(solution)/shard_map/all_gather | solution.py:122
  9.0 518.7 %all-gather.7.cloned.1.call-start = ((), (), s32[]{:S(2)}) async-start(), calls=%async_computation.13 | async-start | bytes 1216512 | tf_op jit(solution)/shard_map/all_gather | solution.py:123
  10.6 610.1 %all-gather.9.cloned.1.call-start = ((), (), s32[]{:S(2)}) async-start(), calls=%async_computation.14 | async-start | bytes 5898240 | tf_op jit(solution)/shard_map/all_gather | solution.py:127
  13.5 619.4 %all-gather.11.cloned.1.call-start = ((), (), s32[]{:S(2)}) async-start(), calls=%async_computation.15 | async-start | bytes 5898240 | tf_op jit(solution)/shard_map/all_gather | solution.py:128
  20.8 294.8 %copy-start.63 = (f32[768]{0:T(1024)}, f32[768]{0:T(1024)S(1)}, u32[]{:S(2)}) copy-start(f32[768]{0:T(1024)S(1)} %get-tuple-element.86) | copy-start | bytes 9220
  144.9 133.9 %copy-start.90 = (bf16[1,32,12]{1,0,2:T(2,128)(2,1)S(1)}, bf16[1,32,12]{1,0,2:T(2,128)(2,1)}, u32[]{:S(2)}) copy-start(bf16[1,32,12]{1,0,2:T(2,128)(2,1)} %get-tuple-element.124) | copy-start | bytes 2308
  144.9 133.9 %copy-start.91 = (bf16[1,32,12]{1,0,2:T(2,128)(2,1)S(1)}, bf16[1,32,12]{1,0,2:T(2,128)(2,1)}, u32[]{:S(2)}) copy-start(bf16[1,32,12]{1,0,2:T(2,128)(2,1)} %get-tuple-element.125) | copy-start | bytes 2308
  144.9 133.9 %copy-start.92 = (bf16[1,32,12]{1,0,2:T(2,128)(2,1)S(1)}, bf16[1,32,12]{1,0,2:T(2,128)(2,1)}, u32[]{:S(2)}) copy-start(bf16[1,32,12]{1,0,2:T(2,128)(2,1)} %get-tuple-element.126) | copy-start | bytes 2308
  313.0 36.1 %collective-permute-start.2 = (bf16[2,512,768]{2,1,0:T(8,128)(2,1)S(1)}, bf16[2,512,768]{2,1,0:T(8,128)(2,1)}, u32[]{:S(2)}, u32[]{:S(2)}) collective-permute-start(bf16[2,512,768]{2,1,0:T(8,128)(2,1)S(1)} %pad_maximum_fusion.5), channel_id=1, source_target_pairs={{0,1},{1,2},{2,3},{4,5},{5,6},{6,7},{8,9},{9,10},{10,11},{12,13},{... | collective-permute-start | bytes 4718600 | tf_op jit(solution)/shard_map/ppermute | solution.py:23
  315.7 39.1 %copy-start.106 = (pred[2,512]{1,0:T(4,128)(4,1)}, pred[2,512]{1,0:T(4,128)(4,1)S(1)}, u32[]{:S(2)}) copy-start(pred[2,512]{1,0:T(4,128)(4,1)S(1)} %broadcast_compare_fusion.2) | copy-start | bytes 3076
  318.8 42.9 %copy-start.26 = (bf16[1,512,768]{2,1,0:T(8,128)(2,1)}, bf16[1,512,768]{2,1,0:T(8,128)(2,1)S(1)}, u32[]{:S(2)}) copy-start(bf16[1,512,768]{2,1,0:T(8,128)(2,1)S(1)} %get-tuple-element.97) | copy-start | bytes 2359300
  318.8 42.9 %copy-start.27 = (bf16[1,512,768]{2,1,0:T(8,128)(2,1)}, bf16[1,512,768]{2,1,0:T(8,128)(2,1)S(1)}, u32[]{:S(2)}) copy-start(bf16[1,512,768]{2,1,0:T(8,128)(2,1)S(1)} %get-tuple-element.98) | copy-start | bytes 2359300
  318.8 69.6 %copy-start.33 = (bf16[2,512,768]{2,1,0:T(8,128)(2,1)S(1)}, bf16[2,512,768]{2,1,0:T(8,128)(2,1)}, u32[]{:S(2)}) copy-start(bf16[2,512,768]{2,1,0:T(8,128)(2,1)} %param.13) | copy-start | bytes 4718596
  319.0 63.8 %collective-permute-start = (bf16[2,512,768]{2,1,0:T(8,128)(2,1)S(1)}, bf16[2,512,768]{2,1,0:T(8,128)(2,1)}, u32[]{:S(2)}, u32[]{:S(2)}) collective-permute-start(bf16[2,512,768]{2,1,0:T(8,128)(2,1)S(1)} %pad_maximum_fusion.4), channel_id=1, source_target_pairs={{0,1},{1,2},{2,3},{4,5},{5,6},{6,7},{8,9},{9,10},{10,11},{12,13},{... | collective-permute-start | bytes 4718600 | tf_op jit(solution)/shard_map/ppermute | solution.py:23
  321.7 68.6 %copy-start.100 = (s32[2,512]{1,0:T(2,128)}, s32[2,512]{1,0:T(2,128)S(1)}, u32[]{:S(2)}) copy-start(s32[2,512]{1,0:T(2,128)S(1)} %get-tuple-element.123) | copy-start | bytes 12292
  321.7 68.6 %copy-start.102 = (s32[2,512]{1,0:T(2,128)}, s32[2,512]{1,0:T(2,128)S(1)}, u32[]{:S(2)}) copy-start(s32[2,512]{1,0:T(2,128)S(1)} %get-tuple-element.122) | copy-start | bytes 12292
  349.1 67.5 %collective-permute-start.3 = (bf16[2,512,768]{2,1,0:T(8,128)(2,1)}, bf16[2,512,768]{2,1,0:T(8,128)(2,1)}, u32[]{:S(2)}, u32[]{:S(2)}) collective-permute-start(bf16[2,512,768]{2,1,0:T(8,128)(2,1)} %collective-permute-done.2), channel_id=1, source_target_pairs={{0,1},{1,2},{2,3},{4,5},{5,6},{6,7},{8,9},{9,10},{10,11},{12,13},{... | collective-permute-start | bytes 4718600 | tf_op jit(solution)/shard_map/ppermute | solution.py:23
  357.2 33.1 %copy-start.104 = (pred[2,512]{1,0:T(4,128)(4,1)}, pred[2,512]{1,0:T(4,128)(4,1)S(1)}, u32[]{:S(2)}) copy-start(pred[2,512]{1,0:T(4,128)(4,1)S(1)} %broadcast_compare_fusion.1) | copy-start | bytes 3076
  382.8 61.9 %collective-permute-start.1 = (bf16[2,512,768]{2,1,0:T(8,128)(2,1)}, bf16[2,512,768]{2,1,0:T(8,128)(2,1)}, u32[]{:S(2)}, u32[]{:S(2)}) collective-permute-start(bf16[2,512,768]{2,1,0:T(8,128)(2,1)} %collective-permute-done), channel_id=1, source_target_pairs={{0,1},{1,2},{2,3},{4,5},{5,6},{6,7},{8,9},{9,10},{10,11},{12,13},{... | collective-permute-start | bytes 4718600 | tf_op jit(solution)/shard_map/ppermute | solution.py:23
  534.1 82.2 %all-to-all-start = ((bf16[8,160,768]{2,1,0:T(8,128)(2,1)}), bf16[8,160,768]{2,1,0:T(8,128)(2,1)}, u32[]{:S(2)}, u32[]{:S(2)}) async-start(bf16[8,160,768]{2,1,0:T(8,128)(2,1)} %bitcast.463), calls=%async_computation | async-start | bytes 3932160 | tf_op jit(solution)/shard_map/all_to_all | solution.py:110
  609.6 431.2 %copy-start.10 = (f32[512,768]{1,0:T(8,128)}, f32[512,768]{1,0:T(8,128)S(1)}, u32[]{:S(2)}) copy-start(f32[512,768]{1,0:T(8,128)S(1)} %get-tuple-element.139) | copy-start | bytes 4718596
  616.3 61.7 %all-to-all-start.4 = ((bf16[8,160,768]{2,1,0:T(8,128)(2,1)}), bf16[8,160,768]{2,1,0:T(8,128)(2,1)}, u32[]{:S(2)}, u32[]{:S(2)}) async-start(bf16[8,160,768]{2,1,0:T(8,128)(2,1)} %bitcast.49), calls=%async_computation.4 | async-start | bytes 3932160 | tf_op jit(solution)/shard_map/all_to_all | solution.py:110
  678.0 83.7 %all-to-all-start.1 = ((bf16[8,2,61440]{2,1,0:T(2,128)(2,1)}), bf16[8,2,61440]{2,1,0:T(2,128)(2,1)S(1)}, u32[]{:S(2)}, u32[]{:S(2)}) async-start(bf16[8,2,61440]{2,1,0:T(2,128)(2,1)} %reshape.782), calls=%async_computation.1 | async-start | bytes 3932160 | tf_op jit(solution)/shard_map/all_to_all | solution.py:114
  763.0 29.7 %all-to-all-start.5 = ((bf16[8,2,61440]{2,1,0:T(2,128)(2,1)}), bf16[8,2,61440]{2,1,0:T(2,128)(2,1)S(1)}, u32[]{:S(2)}, u32[]{:S(2)}) async-start(bf16[8,2,61440]{2,1,0:T(2,128)(2,1)} %reshape.786), calls=%async_computation.5 | async-start | bytes 3932160 | tf_op jit(solution)/shard_map/all_to_all | solution.py:114
  806.2 29.6 %all-to-all-start.2 = ((bf16[8,160,768]{2,1,0:T(8,128)(2,1)}), bf16[8,160,768]{2,1,0:T(8,128)(2,1)}, u32[]{:S(2)}, u32[]{:S(2)}) async-start(bf16[8,160,768]{2,1,0:T(8,128)(2,1)} %bitcast.464), calls=%async_computation.2 | async-start | bytes 3932160 | tf_op jit(solution)/shard_map/all_to_all | solution.py:110
  835.8 29.6 %all-to-all-start.6 = ((bf16[8,160,768]{2,1,0:T(8,128)(2,1)}), bf16[8,160,768]{2,1,0:T(8,128)(2,1)}, u32[]{:S(2)}, u32[]{:S(2)}) async-start(bf16[8,160,768]{2,1,0:T(8,128)(2,1)} %bitcast.465), calls=%async_computation.6 | async-start | bytes 3932160 | tf_op jit(solution)/shard_map/all_to_all | solution.py:110
  840.2 680.5 %reduce-scatter.12.cloned.1.call-start = ((), (), s32[]{:S(2)}) async-start(), calls=%async_computation.19 | async-start | bytes 5898240 | tf_op jit(solution)/shard_map/reduce_scatter | solution.py:408
  945.6 53.3 %all-to-all-start.7 = ((bf16[8,2,61440]{2,1,0:T(2,128)(2,1)}), bf16[8,2,61440]{2,1,0:T(2,128)(2,1)}, u32[]{:S(2)}, u32[]{:S(2)}) async-start(bf16[8,2,61440]{2,1,0:T(2,128)(2,1)} %reshape.784), calls=%async_computation.7 | async-start | bytes 3932160 | tf_op jit(solution)/shard_map/all_to_all | solution.py:114
  998.9 29.6 %all-to-all-start.3 = ((bf16[8,2,61440]{2,1,0:T(2,128)(2,1)}), bf16[8,2,61440]{2,1,0:T(2,128)(2,1)}, u32[]{:S(2)}, u32[]{:S(2)}) async-start(bf16[8,2,61440]{2,1,0:T(2,128)(2,1)} %reshape.780), calls=%async_computation.3 | async-start | bytes 3932160 | tf_op jit(solution)/shard_map/all_to_all | solution.py:114
  1003.2 520.2 %reduce-scatter.10.cloned.1.call-start = ((), (), s32[]{:S(2)}) async-start(), calls=%async_computation.18 | async-start | bytes 5898240 | tf_op jit(solution)/shard_map/reduce_scatter | solution.py:405
  1015.6 510.8 %reduce-scatter.8.cloned.1.call-start = ((), (), s32[]{:S(2)}) async-start(), calls=%async_computation.17 | async-start | bytes 2433024 | tf_op jit(solution)/shard_map/reduce_scatter | solution.py:401
  1046.3 184.4 %copy-start.6 = (f32[512,768]{1,0:T(8,128)}, f32[512,768]{1,0:T(8,128)S(1)}, u32[]{:S(2)}) copy-start(f32[512,768]{1,0:T(8,128)S(1)} %get-tuple-element.104) | copy-start | bytes 4718596
  1136.6 107.1 %collective-permute-start.6 = (bf16[2,512,768]{1,2,0:T(8,128)(2,1)}, bf16[2,512,768]{1,2,0:T(8,128)(2,1)}, u32[]{:S(2)}, u32[]{:S(2)}) collective-permute-start(bf16[2,512,768]{1,2,0:T(8,128)(2,1)} %fusion.85), channel_id=1, source_target_pairs={{1,0},{2,1},{3,2},{5,4},{6,5},{7,6},{9,8},{10,9},{11,10},{13,12},{... | collective-permute-start | bytes 4718600 | tf_op jit(solution)/shard_map/ppermute | solution.py:23
  1229.3 40.8 %collective-permute-start.4 = (bf16[2,512,768]{1,2,0:T(8,128)(2,1)}, bf16[2,512,768]{1,2,0:T(8,128)(2,1)}, u32[]{:S(2)}, u32[]{:S(2)}) collective-permute-start(bf16[2,512,768]{1,2,0:T(8,128)(2,1)} %fusion.90), channel_id=1, source_target_pairs={{1,0},{2,1},{3,2},{5,4},{6,5},{7,6},{9,8},{10,9},{11,10},{13,12},{... | collective-permute-start | bytes 4718600 | tf_op jit(solution)/shard_map/ppermute | solution.py:23
  1233.8 292.6 %reduce-scatter.6.cloned.1.call-start = ((), (), s32[]{:S(2)}) async-start(), calls=%async_computation.16 | async-start | bytes 7299072 | tf_op jit(solution)/shard_map/reduce_scatter | solution.py:400
  1247.8 62.3 %collective-permute-start.7 = (bf16[2,512,768]{1,2,0:T(8,128)(2,1)}, bf16[2,512,768]{1,2,0:T(8,128)(2,1)}, u32[]{:S(2)}, u32[]{:S(2)}) collective-permute-start(bf16[2,512,768]{1,2,0:T(8,128)(2,1)} %fusion.83), channel_id=1, source_target_pairs={{1,0},{2,1},{3,2},{5,4},{6,5},{7,6},{9,8},{10,9},{11,10},{13,12},{... | collective-permute-start | bytes 4718600 | tf_op jit(solution)/shard_map/ppermute | solution.py:23
  1270.0 40.0 %slice-start = ((s8[4718592]{0:T(1024)(128)(4,1)}), s8[4194304]{0:T(1024)(128)(4,1)S(1)}, s32[]{:S(2)}) async-start(s8[4718592]{0:T(1024)(128)(4,1)} %bitcast.421), calls=%async_computation.20 | async-start | bytes 8388608
  1270.0 77.2 %slice-start.2 = ((s8[4718592]{0:T(1024)(128)(4,1)}), s8[4194304]{0:T(1024)(128)(4,1)S(1)}, s32[]{:S(2)}) async-start(s8[4718592]{0:T(1024)(128)(4,1)} %bitcast.426), calls=%async_computation.22 | async-start | bytes 8388608
  1274.3 35.7 %slice-start.1 = ((s8[4718592]{0:T(1024)(128)(4,1)}), s8[524288]{0:T(1024)(128)(4,1)S(1)}, s32[]{:S(2)}) async-start(s8[4718592]{0:T(1024)(128)(4,1)} %bitcast.421), calls=%async_computation.21 | async-start | bytes 1048576
  1274.3 72.9 %slice-start.3 = ((s8[4718592]{0:T(1024)(128)(4,1)}), s8[524288]{0:T(1024)(128)(4,1)S(1)}, s32[]{:S(2)}) async-start(s8[4718592]{0:T(1024)(128)(4,1)} %bitcast.426), calls=%async_computation.23 | async-start | bytes 1048576
  1274.3 72.9 %collective-permute-start.5 = (bf16[2,512,768]{1,2,0:T(8,128)(2,1)}, bf16[2,512,768]{1,2,0:T(8,128)(2,1)}, u32[]{:S(2)}, u32[]{:S(2)}) collective-permute-start(bf16[2,512,768]{1,2,0:T(8,128)(2,1)} %fusion.88), channel_id=1, source_target_pairs={{1,0},{2,1},{3,2},{5,4},{6,5},{7,6},{9,8},{10,9},{11,10},{13,12},{... | collective-permute-start | bytes 4718600 | tf_op jit(solution)/shard_map/ppermute | solution.py:23
  1312.6 41.5 %copy-start.38 = (bf16[512,768]{0,1:T(8,128)(2,1)}, bf16[512,768]{0,1:T(8,128)(2,1)S(1)}, u32[]{:S(2)}) copy-start(bf16[512,768]{0,1:T(8,128)(2,1)S(1)} %get-tuple-element.110) | copy-start | bytes 2359300
  1312.7 41.5 %copy-start.40 = (bf16[512,768]{0,1:T(8,128)(2,1)}, bf16[512,768]{0,1:T(8,128)(2,1)S(1)}, u32[]{:S(2)}) copy-start(bf16[512,768]{0,1:T(8,128)(2,1)S(1)} %get-tuple-element.111) | copy-start | bytes 2359300
  1392.5 32.9 %copy-start.32 = (bf16[512,768]{1,0:T(8,128)(2,1)S(1)}, bf16[512,768]{1,0:T(8,128)(2,1)}, u32[]{:S(2)}) copy-start(bf16[512,768]{1,0:T(8,128)(2,1)} %copy-done.31) | copy-start | bytes 2359300
  1468.4 47.7 %copy-start.95 = (f32[512]{0:T(512)S(1)}, f32[512]{0:T(512)}, u32[]{:S(2)}) copy-start(f32[512]{0:T(512)} %copy-done.94) | copy-start | bytes 6148
  1468.4 47.7 %copy-start.97 = (f32[512]{0:T(512)S(1)}, f32[512]{0:T(512)}, u32[]{:S(2)}) copy-start(f32[512]{0:T(512)} %copy-done.96) | copy-start | bytes 6148
  1468.4 47.8 %copy-start.5 = (f32[512,768]{1,0:T(8,128)S(1)}, f32[512,768]{1,0:T(8,128)}, u32[]{:S(2)}) copy-start(f32[512,768]{1,0:T(8,128)} %copy-done.3) | copy-start | bytes 4718596
  1468.4 47.8 %copy-start.7 = (f32[512,768]{1,0:T(8,128)S(1)}, f32[512,768]{1,0:T(8,128)}, u32[]{:S(2)}) copy-start(f32[512,768]{1,0:T(8,128)} %copy-done.6) | copy-start | bytes 4718596
  (109 other events, 806.2 us)
Sparse Core Ops, SparseCore 0:
  11.4 63.2 all-gather.4
  78.0 52.9 all-gather.6
  132.6 88.3 all-gather.8
  222.3 87.7 all-gather.10
  880.8 83.5 reduce-scatter.11
  1015.7 85.7 reduce-scatter.9
  1233.9 106.0 reduce-scatter.7
  1359.6 120.2 reduce-scatter.5
where the time goes:
time: 1540 us; the launch traced here: 1530 us
  matrix products  535 us (35%)
  local copies, waits for them, and re-layouts  351 us (23%)
  other arithmetic  261 us (17%)
  waiting for transfers between devices  196 us (13%)
  blocking collectives  117 us (8%)
  starting transfers between devices  57.3 us (4%)
  between operations  16.4 us (1%)
    ppermute x8, waiting for transfers between devices, passed_along(): return lax.ppermute(block, axis, route)  162 us
    eq x1, local copies, waits for them, and re-layouts, on_device(): bucket_ids[..., None] == jnp.arange(NB, dtype=jnp.int32)  134 us
    dot_general x2, matrix products, score_block(): jnp.einsum('qhd,khd->hqk', queries, key_buf, preferred_element_type=jnp.f...  75 us
    all_gather x1, blocking collectives, fetch_weights(): lax.all_gather(router_part, ('dp', 'ctx'), axis=1, tiled=True)  74.5 us
    convert_element_type x2, local copies, waits for them, and re-layouts, attend_backward(): grad_scores = (soft_probs * (grad_probs - inner_sum)).astype(jnp.bfloat16)  63.3 us
    convert_element_type x2, other arithmetic, attend_backward(): grad_scores = (soft_probs * (grad_probs - inner_sum)).astype(jnp.bfloat16)  62.7 us
    unnamed x279, local copies, waits for them, and re-layouts  57.1 us
    unnamed x8, other arithmetic  54.4 us
  transfers between devices with their start and end apart: 24, of which 10 were waited for; matrix products, arithmetic and copies ran while one was open for 72% of the time, Pallas kernels for 0%

commit v1 on v0

v1 whole, which is shorter than its diff:
```python
from functools import partial

import jax
import jax.numpy as jnp
from jax import lax
from jax.experimental import pallas as pl
from jax.experimental.pallas import tpu as pltpu
from jax.sharding import PartitionSpec as P

HEADS=12; HEAD_DIM=64; NB=32; WIN=1024; TOP=2
NEG=-1e30
BUCKET_EDGES = [16, 21, 27, 35, 45, 58, 76, 98, 128, 166, 215, 279, 362, 470, 609, 790]
QB=256; CB=256; SPAN=WIN+QB; GROWS=SPAN+128; GSEG=GROWS//128

NT=(((1,),(1,)),((),()))
NN=(((1,),(0,)),((),()))
def dot(a,b,dims): return lax.dot_general(a,b,dims,preferred_element_type=jnp.float32)

def bucket_index(distance):
    edge_values = jnp.array(BUCKET_EDGES, dtype=jnp.int32)
    passed = jnp.sum((distance[..., None] >= edge_values).astype(jnp.int32), axis=-1)
    return jnp.where(distance < 16, distance, 15 + passed)

def bias_line(table):
    n = GROWS + 128
    d = jnp.arange(n, dtype=jnp.int32) - 256
    hot = (jnp.clip(bucket_index(d),0,NB-1)[:,None]==jnp.arange(NB)).astype(jnp.float32)
    line = jnp.einsum("nb,bh->hn", hot, table, precision=lax.Precision.HIGHEST)
    line = jnp.where((d>=0)&(d<WIN), line, NEG)
    return line.reshape(HEADS//2,2,n)

def spread_bias(line_ref, g_ref):
    for hh in range(2):
        for a in range(GSEG):
            start = (GSEG-1-a)*128
            seg = line_ref[0, hh:hh+1, start:start+256]
            x = jnp.broadcast_to(seg,(128,256))
            x = pltpu.roll(x,0,1,stride=1,stride_axis=0)
            g_ref[hh, a*128:(a+1)*128,:] = x[:,128:256]

def bias_chunk(g_ref, hh, r):
    o = pl.multiple_of(r*CB,CB) if not isinstance(r,int) else r*CB
    return jnp.concatenate([g_ref[hh, pl.ds(o+128,CB),:], g_ref[hh, pl.ds(o,CB),:]],axis=1)

def rows8(x, op):
    return op(x.reshape(x.shape[0]//8,8,x.shape[1]),axis=0)

def fwd_kernel(c0, line_ref, q_ref, k_ref, v_ref, qf_ref, kf_ref, o_ref, lse_ref, g_ref, kh_ref, qh_ref, vt_ref, s_ref, ot_ref):
    T=q_ref.shape[1]
    @pl.when(pl.program_id(1)==0)
    def _(): spread_bias(line_ref,g_ref)
    lane = lax.broadcasted_iota(jnp.int32,(1,128),1)
    vt_ref[...] = v_ref[0].T
    for hh in range(2):
        mine = (lane//64)==hh
        kh_ref[...] = jnp.where(mine,k_ref[0],kf_ref[0])
        qh_ref[...] = jnp.where(mine,q_ref[0],qf_ref[0])
        for b in range(T//QB):
            qb = qh_ref[b*QB:(b+1)*QB,:]
            mx=None
            for r in range(SPAN//CB):
                base=b*QB+c0+r*CB
                s=dot(kh_ref[base:base+CB,:],qb,NT)+bias_chunk(g_ref,hh,r)
                s_ref[r]=s
                m8=rows8(s,jnp.max)
                mx=m8 if mx is None else jnp.maximum(mx,m8)
            m=jnp.max(mx,axis=0,keepdims=True)
            tot=None; acc=None
            for r in range(SPAN//CB):
                base=b*QB+c0+r*CB
                p=jnp.exp(s_ref[r]-m)
                t8=rows8(p,jnp.sum)
                tot=t8 if tot is None else tot+t8
                d=dot(vt_ref[64*hh:64*hh+64,base:base+CB],p.astype(jnp.bfloat16),NN)
                acc=d if acc is None else acc+d
            l=jnp.sum(tot,axis=0,keepdims=True)
            ot_ref[64*hh:64*hh+64,b*QB:(b+1)*QB]=acc*(1.0/l)
            lse_ref[0,0,hh:hh+1,b*QB:(b+1)*QB]=m+jnp.log(l)
    o_ref[0]=ot_ref[...].T.astype(jnp.bfloat16)

def attn_forward(line,q,kv,qf,kf,c0):
    B,T,D=q.shape; K=kv.shape[1]; PR=D//128
    return pl.pallas_call(
        partial(fwd_kernel,c0),
        grid=(PR,B),
        in_specs=[pl.BlockSpec((1,2,line.shape[2]),lambda p,m:(p,0,0)),
                  pl.BlockSpec((1,T,128),lambda p,m:(m,0,p)),
                  pl.BlockSpec((1,K,128),lambda p,m:(m,0,p)),
                  pl.BlockSpec((1,K,128),lambda p,m:(m,0,PR+p)),
                  pl.BlockSpec((1,T,128),lambda p,m:(m,0,0)),
                  pl.BlockSpec((1,K,128),lambda p,m:(m,0,0))],
        out_specs=[pl.BlockSpec((1,T,128),lambda p,m:(m,0,p)),
                   pl.BlockSpec((1,1,2,T),lambda p,m:(m,p,0,0))],
        out_shape=[jax.ShapeDtypeStruct((B,T,D),jnp.bfloat16),jax.ShapeDtypeStruct((B,PR,2,T),jnp.float32)],
        scratch_shapes=[pltpu.VMEM((2,GROWS,128),jnp.float32),pltpu.VMEM((K,128),jnp.bfloat16),pltpu.VMEM((T,128),jnp.bfloat16),
                        pltpu.VMEM((128,K),jnp.bfloat16),pltpu.VMEM((SPAN//CB,CB,QB),jnp.float32),pltpu.VMEM((128,T),jnp.float32)],
        cost_estimate=pl.CostEstimate(flops=4*B*D*T*SPAN,bytes_accessed=2*B*D*(2*T+2*K),transcendentals=B*HEADS*T*SPAN),
    )(line,q,kv,kv,qf,kf)

def bwd_kernel(c0, line_ref, q_ref, k_ref, v_ref, g_ref_in, qf_ref, kf_ref, lse_ref, dl_ref, dq_ref, dk_ref, dv_ref, tg_ref,
               g_ref, kh_ref, qh_ref, qz_ref, dz_ref, kt_ref, dk_acc, dv_acc, dqt_acc, t_acc):
    T=q_ref.shape[1]
    last=pl.num_programs(1)-1
    @pl.when(pl.program_id(1)==0)
    def _():
        spread_bias(line_ref,g_ref)
        t_acc[...]=jnp.zeros_like(t_acc)
    lane = lax.broadcasted_iota(jnp.int32,(1,128),1)
    kt_ref[...] = k_ref[0].T
    dk_acc[...]=jnp.zeros_like(dk_acc)
    dv_acc[...]=jnp.zeros_like(dv_acc)
    for hh in range(2):
        mine = (lane//64)==hh
        kh_ref[hh] = jnp.where(mine,k_ref[0],kf_ref[0])
        qh_ref[hh] = jnp.where(mine,q_ref[0],qf_ref[0])
        qz_ref[hh] = jnp.where(mine,q_ref[0],jnp.zeros_like(q_ref[0]))
        dz_ref[hh] = jnp.where(mine,g_ref_in[0],jnp.zeros_like(q_ref[0]))
    dqt_acc[...]=jnp.zeros_like(dqt_acc)
    nb=T//QB
    def step(r,carry):
        for b in range(nb):
            for hh in range(2):
                base=pl.multiple_of(b*QB+c0+r*CB,128)
                keys=pl.ds(base,CB)
                rows=slice(b*QB,(b+1)*QB)
                s=dot(kh_ref[hh,keys,:],qh_ref[hh,rows,:],NT)+bias_chunk(g_ref,hh,r)
                p=jnp.exp(s-lse_ref[0,0,hh:hh+1,rows])
                dp=dot(v_ref[0,keys,:],dz_ref[hh,rows,:],NT)
                ds=p*(dp-dl_ref[0,0,hh:hh+1,rows])
                dsb=ds.astype(jnp.bfloat16)
                dv_acc[keys,:]+=dot(p.astype(jnp.bfloat16),dz_ref[hh,rows,:],NN)
                dk_acc[keys,:]+=dot(dsb,qz_ref[hh,rows,:],NN)
                dqt_acc[64*hh:64*hh+64,rows]+=dot(kt_ref[64*hh:64*hh+64,keys],dsb,NN)
                o=pl.multiple_of(r*CB,CB)
                t_acc[hh,pl.ds(o+128,CB),:]+=ds[:,:128]
                t_acc[hh,pl.ds(o,CB),:]+=ds[:,128:]
        return carry
    lax.fori_loop(0,SPAN//CB,step,0)
    dk_ref[0]=dk_acc[...].astype(jnp.bfloat16)
    dv_ref[0]=dv_acc[...].astype(jnp.bfloat16)
    dq_ref[0]=(dqt_acc[...].T*(HEAD_DIM**-0.5)).astype(jnp.bfloat16)
    @pl.when(pl.program_id(1)==last)
    def _():
        flip=(lax.broadcasted_iota(jnp.int32,(128,128),0)+lax.broadcasted_iota(jnp.int32,(128,128),1)==127).astype(jnp.float32)
        for hh in range(2):
            for a in range(GSEG):
                blk=lax.dot_general(flip,t_acc[hh,a*128:(a+1)*128,:],NN,precision=lax.Precision.HIGHEST,preferred_element_type=jnp.float32)
                x=jnp.concatenate([blk,jnp.zeros_like(blk)],axis=1)
                x=pltpu.roll(x,0,1,stride=1,stride_axis=0)
                tg_ref[0,hh,a:a+1,:]=jnp.sum(x,axis=0,keepdims=True)

def attn_backward(line,q,kv,do,qf,kf,lse,dl,c0):
    B,T,D=q.shape; K=kv.shape[1]; PR=D//128
    return pl.pallas_call(
        partial(bwd_kernel,c0),
        grid=(PR,B),
        in_specs=[pl.BlockSpec((1,2,line.shape[2]),lambda p,m:(p,0,0)),
                  pl.BlockSpec((1,T,128),lambda p,m:(m,0,p)),
                  pl.BlockSpec((1,K,128),lambda p,m:(m,0,p)),
                  pl.BlockSpec((1,K,128),lambda p,m:(m,0,PR+p)),
                  pl.BlockSpec((1,T,128),lambda p,m:(m,0,p)),
                  pl.BlockSpec((1,T,128),lambda p,m:(m,0,0)),
                  pl.BlockSpec((1,K,128),lambda p,m:(m,0,0)),
                  pl.BlockSpec((1,1,2,T),lambda p,m:(m,p,0,0)),
                  pl.BlockSpec((1,1,2,T),lambda p,m:(m,p,0,0))],
        out_specs=[pl.BlockSpec((1,T,128),lambda p,m:(m,0,p)),
                   pl.BlockSpec((1,K,128),lambda p,m:(m,0,p)),
                   pl.BlockSpec((1,K,128),lambda p,m:(m,0,p)),
                   pl.BlockSpec((1,2,GSEG,256),lambda p,m:(p,0,0,0))],
        out_shape=[jax.ShapeDtypeStruct((B,T,D),jnp.bfloat16),jax.ShapeDtypeStruct((B,K,D),jnp.bfloat16),
                   jax.ShapeDtypeStruct((B,K,D),jnp.bfloat16),jax.ShapeDtypeStruct((PR,2,GSEG,256),jnp.float32)],
        scratch_shapes=[pltpu.VMEM((2,GROWS,128),jnp.float32),pltpu.VMEM((2,K,128),jnp.bfloat16),pltpu.VMEM((2,T,128),jnp.bfloat16),
                        pltpu.VMEM((2,T,128),jnp.bfloat16),pltpu.VMEM((2,T,128),jnp.bfloat16),pltpu.VMEM((128,K),jnp.bfloat16),
                        pltpu.VMEM((K,128),jnp.float32),pltpu.VMEM((K,128),jnp.float32),pltpu.VMEM((128,T),jnp.float32),
                        pltpu.VMEM((2,GROWS,128),jnp.float32)],
        cost_estimate=pl.CostEstimate(flops=10*B*D*T*SPAN,bytes_accessed=2*B*D*(2*T+2*K)*2,transcendentals=B*HEADS*T*SPAN),
    )(line,q,kv,kv,do,qf,kf,lse,dl)

def table_from_diagonals(diag):
    d = WIN+128-128*jnp.arange(GSEG)[:,None]+(jnp.arange(256)[None,:]-127)
    hot=(jnp.clip(bucket_index(d),0,NB-1)[...,None]==jnp.arange(NB)).astype(jnp.float32)
    hot=hot*((d>=0)&(d<WIN)).astype(jnp.float32)[...,None]
    h=diag.reshape(HEADS,GSEG*256)
    return jnp.einsum("hn,nb->bh",h,hot.reshape(GSEG*256,NB),precision=lax.Precision.HIGHEST)

def features(qdoc,kdoc,kvalid):
    lane=jnp.arange(128)%64
    qf=(qdoc[...,None]==lane).astype(jnp.bfloat16)
    bad=(kdoc[...,None]!=lane)|~kvalid[...,None]
    kf=jnp.where(bad&(lane<8),NEG,0.0).astype(jnp.bfloat16)
    return qf,kf


GELU_C = 0.7978845608028654
GELU_A = 0.044715


def row_step(rows):
    for size in (256, 128, 64, 32, 16):
        if rows % size == 0:
            return size
    return rows


def expert_kernel(with_prior, xg_ref, up_ref, dn_ref, *refs):
    if with_prior:
        pu_ref, pd_ref, ret_ref, ug_ref, dg_ref, acc, xt, gt, hb, zb = refs
    else:
        ret_ref, ug_ref, dg_ref, acc, xt, gt, hb, zb = refs
    R = xg_ref.shape[0]
    D = xg_ref.shape[1] // 2
    RB = row_step(R)

    @pl.when(pl.program_id(0) == 0)
    def _():
        xt[...] = xg_ref[:, :D].T
        gt[...] = xg_ref[:, D:].T
        acc[...] = jnp.zeros_like(acc)

    up = up_ref[...]
    dn = dn_ref[...]

    def block(i, carry):
        rs = pl.ds(pl.multiple_of(i * RB, RB), RB)
        z = dot(xg_ref[rs, :D], up, NN)
        dh = dot(xg_ref[rs, D:], dn, NT)
        zz = z * z
        t = jnp.tanh(z * (GELU_C + (GELU_C * GELU_A) * zz))
        half = 0.5 + 0.5 * t
        h = (z * half).astype(jnp.bfloat16)
        slope = half + z * (0.5 - 0.5 * t * t) * (GELU_C + (3.0 * GELU_C * GELU_A) * zz)
        dz = (dh * slope).astype(jnp.bfloat16)
        hb[rs, :] = h
        zb[rs, :] = dz
        acc[rs, :D] += dot(h, dn, NN)
        acc[rs, D:] += dot(dz, up, NT)
        return carry

    lax.fori_loop(0, R // RB, block, 0)
    ug = dot(xt[...], zb[...], NN)
    dg = dot(gt[...], hb[...], NN)
    if with_prior:
        ug += pu_ref[...]
        dg += pd_ref[...]
    ug_ref[...] = ug.astype(ug_ref.dtype)
    dg_ref[...] = dg.astype(dg_ref.dtype)

    @pl.when(pl.program_id(0) == pl.num_programs(0) - 1)
    def _():
        ret_ref[...] = acc[...].astype(jnp.bfloat16)


def expert_step(xg, up, dn, prior, last):
    R, D2 = xg.shape
    D, F = up.shape
    FC = 512
    wide = pl.BlockSpec((D, FC), lambda f: (0, f))
    tall = pl.BlockSpec((FC, D), lambda f: (f, 0))
    whole = pl.BlockSpec((R, D2), lambda f: (0, 0))
    grad_type = jnp.bfloat16 if last else jnp.float32
    return pl.pallas_call(
        partial(expert_kernel, prior is not None),
        grid=(F // FC,),
        in_specs=[whole, wide, tall] + ([wide, wide] if prior is not None else []),
        out_specs=[whole, wide, wide],
        out_shape=[
            jax.ShapeDtypeStruct((R, D2), jnp.bfloat16),
            jax.ShapeDtypeStruct((D, F), grad_type),
            jax.ShapeDtypeStruct((D, F), grad_type),
        ],
        scratch_shapes=[
            pltpu.VMEM((R, D2), jnp.float32),
            pltpu.VMEM((D, R), jnp.bfloat16),
            pltpu.VMEM((D, R), jnp.bfloat16),
            pltpu.VMEM((R, FC), jnp.bfloat16),
            pltpu.VMEM((R, FC), jnp.bfloat16),
        ],
        cost_estimate=pl.CostEstimate(
            flops=12 * R * D * F, bytes_accessed=8 * D * F + 8 * R * D, transcendentals=R * F
        ),
    )(xg, up, dn, *(prior if prior is not None else ()))


EPS = 1e-06


def passed_along(block, axis, distance):
    devices = range(lax.axis_size(axis))
    route = [(i - distance, i) for i in devices if i - distance in devices]
    return lax.ppermute(block, axis, route)


def rms_norm(operand, gain_vec):
    return operand * lax.rsqrt(jnp.mean(operand * operand, axis=-1, keepdims=True) + EPS) * gain_vec


def doc_of(positions, lengths):
    bounds = jnp.cumsum(lengths)[:-1]
    return jnp.sum((positions[:, None] >= bounds[None, :]).astype(jnp.int32), axis=-1)


def gate_values(logits, route_picks):
    soft_probs = jax.nn.softmax(logits, axis=-1)
    chosen = jnp.sum(soft_probs[:, None, :] * route_picks, axis=-1)
    return chosen / jnp.sum(chosen, axis=-1, keepdims=True)


def exchange(payload, ranks):
    shape = payload.shape
    blocks = payload.reshape(ranks, shape[0] // ranks, shape[1])
    return lax.all_to_all(blocks, "dp", split_axis=0, concat_axis=0, tiled=True).reshape(shape)


def mm(a, b):
    return jnp.dot(a, b, preferred_element_type=jnp.float32)


def on_device(
    tokens,
    cotangent,
    proj_weights,
    out_weights,
    router_weights,
    norm_gains,
    bias_table,
    up_weights,
    down_weights,
    doc_lengths,
    routes,
):
    B, T, D = tokens.shape
    low = jnp.bfloat16
    ranks = lax.axis_size("dp")
    experts = ranks * up_weights.shape[1]
    capacity = max(2, 5 * TOP * T // (4 * experts))
    slots = experts * capacity
    hops = (WIN + T - 2) // T
    K = (hops + 1) * T
    c0 = K - T - WIN
    base_pos = lax.axis_index("ctx") * T

    x_own = tokens
    pieces = [x_own]
    moving = x_own
    for _ in range(hops):
        moving = passed_along(moving, "ctx", 1)
        pieces.append(moving)
    x_all = jnp.concatenate(pieces[::-1], axis=1)

    router_pad = jnp.pad(router_weights[0], ((0, 0), (0, 128 - experts)))
    dense = jnp.concatenate([proj_weights[0], out_weights[0], router_pad], axis=1).astype(low)
    dense_full = lax.all_gather(dense, ("dp", "ctx"), axis=0, tiled=True)
    up_full = lax.all_gather(up_weights[0, 0].astype(low), "ctx", axis=1, tiled=True)
    dn_full = lax.all_gather(down_weights[0, 0].astype(low), "ctx", axis=0, tiled=True)
    w_q, w_k, w_v = (dense_full[:, i * D : (i + 1) * D] for i in range(3))
    w_kv = dense_full[:, D : 3 * D]
    w_out = dense_full[:, 3 * D : 4 * D]
    w_router = dense_full[:, 4 * D : 4 * D + experts]
    gains = norm_gains[0]

    line = bias_line(bias_table[0])
    rows = jnp.arange(T, dtype=jnp.int32)
    key_pos = base_pos - (K - T) + jnp.arange(K, dtype=jnp.int32)
    key_doc = jnp.stack([doc_of(key_pos, doc_lengths[m]) for m in range(B)])
    key_ok = jnp.broadcast_to(key_pos >= 0, (B, K))
    qf, kf = features(key_doc[:, K - T :], key_doc, key_ok)

    normed = rms_norm(x_all.astype(jnp.float32), gains[0]).astype(low)
    kv = mm(normed.reshape(B * K, D), w_kv).astype(low).reshape(B, K, 2 * D)
    normed_own = normed[:, K - T :]
    q = (mm(normed_own.reshape(B * T, D), w_q).astype(low) * low(HEAD_DIM**-0.5)).reshape(B, T, D)

    attn, lse = attn_forward(line, q, kv, qf, kf, c0)

    expert_ids = jnp.arange(experts, dtype=jnp.int32)
    slot_range = jnp.arange(slots, dtype=jnp.int32)
    kept = []
    for m in range(B):
        route_now = routes[m]
        picks = (route_now[:, :, None] == expert_ids).astype(jnp.float32)
        order_hot = (jnp.transpose(route_now).reshape(-1)[:, None] == expert_ids[None, :]).astype(
            jnp.int32
        )
        running = jnp.cumsum(order_hot, axis=0)
        slot_pos = (jnp.sum(running * order_hot, axis=-1) - 1).reshape(TOP, T)
        slot_ids = jnp.transpose(route_now) * capacity + slot_pos
        slot_ids = jnp.where(slot_pos < capacity, slot_ids, slots)
        hot = slot_ids[:, None, :] == slot_range[None, :, None]
        table = (hot[0] | hot[1]).astype(low)

        resid = tokens[m].astype(jnp.float32)
        d_out = cotangent[m]
        middle = resid + mm(attn[m], w_out)
        two_low = rms_norm(middle, gains[1]).astype(low)
        logits = mm(two_low, w_router)
        gates = gate_values(logits, picks)
        slot_gate = jnp.sum(
            jnp.where(hot[0], gates[None, :, 0], 0.0) + jnp.where(hot[1], gates[None, :, 1], 0.0),
            axis=1,
        )
        sent = mm(table, jnp.concatenate([two_low, d_out], axis=1))
        d_rows = sent[:, D:].astype(low)
        payload = jnp.concatenate(
            [sent[:, :D].astype(low), (sent[:, D:] * slot_gate[:, None]).astype(low)], axis=1
        )
        received = exchange(payload, ranks)
        kept.append((picks, hot, table, middle, two_low, logits, slot_gate, d_rows, received))

    prior = None
    returned = []
    for m in range(B):
        last = m == B - 1
        back, up_part, dn_part = expert_step(kept[m][-1], up_full, dn_full, prior, last)
        prior = (up_part, dn_part)
        returned.append(exchange(back, ranks))
    up_part, dn_part = prior
    up_grad = lax.psum_scatter(up_part, "ctx", scatter_dimension=1, tiled=True)
    dn_grad = lax.psum_scatter(dn_part, "ctx", scatter_dimension=1, tiled=True)

    outputs = []
    mids = []
    d_branches = []
    d_attns = []
    router_grad = 0.0
    gain_two = 0.0
    for m in range(B):
        picks, hot, table, middle, two_low, logits, slot_gate, d_rows, _ = kept[m]
        back = returned[m]
        d_resid = cotangent[m].astype(jnp.float32)
        slot_dgate = jnp.sum(d_rows.astype(jnp.float32) * back[:, :D].astype(jnp.float32), axis=1)
        d_gates = jnp.stack(
            [jnp.sum(jnp.where(hot[k], slot_dgate[:, None], 0.0), axis=0) for k in range(TOP)], axis=1
        )
        scaled = (back[:, :D].astype(jnp.float32) * slot_gate[:, None]).astype(low)
        joined = jnp.concatenate([scaled, back[:, D:]], axis=1)
        gathered = lax.dot_general(
            table, joined, (((0,), (0,)), ((), ())), preferred_element_type=jnp.float32
        )
        outputs.append((middle + gathered[:, :D]).astype(low))
        gate_pull = jax.vjp(partial(gate_values, route_picks=picks), logits)[1]
        d_logits = gate_pull(d_gates)[0].astype(low)
        router_grad = router_grad + mm(two_low.T, d_logits)
        d_two = gathered[:, D:] + mm(d_logits, w_router.T)
        d_norm, gain_part = jax.vjp(rms_norm, middle, gains[1])[1](d_two)
        gain_two = gain_two + gain_part
        d_mid = d_resid + d_norm
        d_branch = d_mid.astype(low)
        mids.append(d_mid)
        d_branches.append(d_branch)
        d_attns.append(mm(d_branch, w_out.T).astype(low))
    d_attn = jnp.stack(d_attns)
    d_branch = jnp.concatenate(d_branches)
    out_grad = mm(attn.reshape(B * T, D).T, d_branch)
    delta = jnp.sum(
        (attn.astype(jnp.float32) * d_attn.astype(jnp.float32)).reshape(B, T, HEADS, HEAD_DIM), axis=-1
    )
    delta = jnp.transpose(delta, (0, 2, 1)).reshape(B, HEADS // 2, 2, T)
    dq, dk, dv, diag = attn_backward(line, q, kv, d_attn, qf, kf, lse, delta, c0)
    table_grad = table_from_diagonals(diag)

    d_normed = (mm(dk.reshape(B * K, D), w_k.T) + mm(dv.reshape(B * K, D), w_v.T)).reshape(B, K, D)
    carried = d_normed[:, :T]
    for hop in range(hops - 1, -1, -1):
        start = (hops - hop) * T
        carried = (
            passed_along(carried.astype(low), "ctx", -1).astype(jnp.float32)
            + d_normed[:, start : start + T]
        )
    own = carried + mm(dq.reshape(B * T, D), w_q.T).reshape(B, T, D)
    normed_rows = normed.reshape(B * K, D)
    proj_grad = jnp.concatenate(
        [
            mm(normed_own.reshape(B * T, D).T, dq.reshape(B * T, D)),
            mm(normed_rows.T, dk.reshape(B * K, D)),
            mm(normed_rows.T, dv.reshape(B * K, D)),
        ],
        axis=1,
    ).astype(low)
    d_first, gain_one = jax.vjp(rms_norm, tokens.astype(jnp.float32), gains[0])[1](own)
    tokens_grad = (jnp.stack(mids) + d_first).astype(low)

    side = jnp.concatenate(
        [out_grad, jnp.pad(router_grad, ((0, 0), (0, 128 - experts)))], axis=1
    ).astype(low)
    side_part = lax.psum_scatter(side, ("dp", "ctx"), scatter_dimension=0, tiled=True)
    proj_part = lax.psum_scatter(proj_grad, ("dp", "ctx"), scatter_dimension=0, tiled=True)
    gains_total, table_total = lax.psum(
        (jnp.stack([gain_one, gain_two])[None], table_grad[None]), ("dp", "ctx")
    )
    wide = jnp.float32
    return (
        jnp.stack(outputs),
        tokens_grad,
        proj_part.astype(wide)[None],
        side_part[:, :D].astype(wide)[None],
        side_part[:, D : D + experts].astype(wide)[None],
        gains_total,
        table_total,
        up_grad.astype(wide)[None, None],
        dn_grad.astype(wide).T[None, None],
    )


def solution(mesh):
    in_specs = (
        P("dp", "ctx", None),
        P("dp", "ctx", None),
        P(None, ("dp", "ctx"), None),
        P(None, ("dp", "ctx"), None),
        P(None, ("dp", "ctx"), None),
        P(),
        P(),
        P(None, "dp", None, "ctx"),
        P(None, "dp", "ctx", None),
        P("dp", None),
        P("dp", "ctx", None),
    )
    out_specs = (
        P("dp", "ctx", None),
        P("dp", "ctx", None),
        P(None, ("dp", "ctx"), None),
        P(None, ("dp", "ctx"), None),
        P(None, ("dp", "ctx"), None),
        P(),
        P(),
        P(None, "dp", None, "ctx"),
        P(None, "dp", "ctx", None),
    )
    return jax.shard_map(
        on_device, mesh=mesh, in_specs=in_specs, out_specs=out_specs, check_vma=False
    )
```

time: 1540 us -> 1010 us (0.66)
  matrix products: 535 us -> 76.9 us
  local copies, waits for them, and re-layouts: 351 us -> 35.7 us
  Pallas kernels: 0 us -> 246 us
  waiting for transfers between devices: 196 us -> 432 us
  other arithmetic: 261 us -> 75.2 us
  starting transfers between devices: 57.3 us -> 28.1 us
  blocking collectives: 117 us -> 99.4 us
    dot_general x53 -> x25, matrix products: 535 us -> 76.9 us  [the longest x21 70.9 us: mm(): return jnp.dot(a, b, preferred_element_type=jnp.float32)]
    pallas_call x0 -> x4, Pallas kernels: none -> 246 us  [the longest x2 109 us: expert_step(): pl.pallas_call(partial(expert_kernel, prior is not None), grid=(F // FC,)...]
    eq x2 -> x0, local copies, waits for them, and re-layouts: 134 us -> none  [the longest x1 134 us: on_device(): bucket_ids[..., None] == jnp.arange(NB, dtype=jnp.int32)]
    reduce_scatter x4 -> x2, waiting for transfers between devices: 0.01 us -> 125 us  [the longest x1 82.1 us: on_device(): up_grad = lax.psum_scatter(up_part, 'ctx', scatter_dimension=1, tiled=True)]
    convert_element_type x9 -> x0, local copies, waits for them, and re-layouts: 125 us -> none  [the longest x2 63.3 us: attend_backward(): grad_scores = (soft_probs * (grad_probs - inner_sum)).astype(jnp.bfloat16)]
    all_gather x1 -> x0, blocking collectives: 74.5 us -> none  [fetch_weights(): lax.all_gather(router_part, ('dp', 'ctx'), axis=1, tiled=True)]
    convert_element_type x18 -> x16, other arithmetic: 92.4 us -> 23.7 us  [the longest x3 6.13 us: on_device(): normed = rms_norm(x_all.astype(jnp.float32), gains[0]).astype(low)]
    all_gather x4 -> x3, waiting for transfers between devices: 0.06 us -> 67.5 us  [the longest x1 67.4 us: on_device(): lax.all_gather(down_weights[0, 0].astype(low), 'ctx', axis=0, tiled=True)]
  transfers between devices with their start and end apart: 24 -> 14, of which waited for: 10 -> 9; matrix products, arithmetic and copies ran while one was open for 72% -> 13% of each run, Pallas kernels for 0% -> 14%
where the time goes in v1:
time: 1010 us
  waiting for transfers between devices  432 us (43%)
  Pallas kernels  246 us (24%)
  blocking collectives  99.4 us (10%)
  matrix products  76.9 us (8%)
  other arithmetic  75.2 us (7%)
  local copies, waits for them, and re-layouts  35.7 us (4%)
  starting transfers between devices  28.1 us (3%)
  between operations  15.7 us (2%)
    ppermute x4, waiting for transfers between devices, passed_along(): return lax.ppermute(block, axis, route)  151 us
    pallas_call x2, Pallas kernels, expert_step(): pl.pallas_call(partial(expert_kernel, prior is not None), grid=(F // FC,)...  109 us
    pallas_call x1, Pallas kernels, attn_backward(): pl.pallas_call(partial(bwd_kernel, c0), grid=(PR, B), in_specs=[pl.BlockS...  93.9 us
    all_to_all x3, waiting for transfers between devices, exchange(): lax.all_to_all(blocks, 'dp', split_axis=0, concat_axis=0, tiled=True)  87.7 us
    reduce_scatter x1, waiting for transfers between devices, on_device(): up_grad = lax.psum_scatter(up_part, 'ctx', scatter_dimension=1, tiled=True)  82.1 us
    dot_general x21, matrix products, mm(): return jnp.dot(a, b, preferred_element_type=jnp.float32)  70.9 us
    all_gather x1, waiting for transfers between devices, on_device(): lax.all_gather(down_weights[0, 0].astype(low), 'ctx', axis=0, tiled=True)  67.4 us
    psum x1, blocking collectives, on_device(): lax.psum((jnp.stack([gain_one, gain_two])[None], table_grad[None]), ('dp'...  49.7 us
  transfers between devices with their start and end apart: 14, of which 9 were waited for; matrix products, arithmetic and copies ran while one was open for 13% of the time, Pallas kernels for 14%

profile of v1, /device:TPU:0, one launch (start us, length us, event | category | flops | bytes accessed | tf_op | source)
XLA Modules:
  0.0 1009.5 jit_solution(6421948104094073583)
XLA Ops:
  10.6 2.8 convert_element_type.207
  13.5 5.1 collective-permute-start
  18.6 2.8 convert_element_type.209
  30.2 2.6 slice_bitcast_fusion.5
  32.8 32.3 %collective-permute-done = bf16[2,512,768]{2,1,0:T(8,128)(2,1)S(1)} collective-permute-done((bf16[2,512,768]{2,1,0:T(8,128)(2,1)S(1)}, bf16[2,512,768]{2,1,0:T(8,128)(2,1)S(1)}, u32[]{:S(2)}, u32[]{:S(2)}) %collective-permute-start) | collective-permute-done | bytes 1572896 | tf_op jit(solution)/shard_map/ppermute | solution.py:290
  65.1 6.1 collective-permute-start.1
  73.4 3.2 iota_compare_fusion
  76.5 47.9 %collective-permute-done.1 = bf16[2,512,768]{2,1,0:T(8,128)(2,1)S(1)} collective-permute-done((bf16[2,512,768]{2,1,0:T(8,128)(2,1)S(1)}, bf16[2,512,768]{2,1,0:T(8,128)(2,1)S(1)}, u32[]{:S(2)}, u32[]{:S(2)}) %collective-permute-start.1) | collective-permute-done | bytes 1572896 | tf_op jit(solution)/shard_map/ppermute | solution.py:290
  133.9 3.0 fusion.1
  136.9 4.0 fusion.44
  140.9 11.2 %convolution_convert_fusion = bf16[3072,1536]{1,0:T(8,128)(2,1)} fusion(bf16[3072,768]{1,0:T(8,128)(2,1)S(1)} %copy-done.19, bf16[768,3200]{1,0:T(8,128)(2,1)} %all-gather.6.cloned.1.call-done), kind=kOutput, calls=%fused_computation | convolution fusion | flops 7252475904 | bytes 16515072 | tf_op jit(solution)/shard_map/dot_general | solution.py:315
  152.1 43.3 %shard_map.196 = (bf16[2,512,768]{2,1,0:T(8,128)(2,1)}, f32[2,6,2,512]{3,2,1,0:T(2,128)}) custom-call(f32[6,2,1536]{2,1,0:T(2,128)} %reshape.436.line_ref, bf16[2,512,768]{2,1,0:T(8,128)(2,1)} %bitcast.297, bf16[2,1536,1536]{2,1,0:T(8,128)(2,1)} %bitcast.289, bf16[2,1536,1536]{2,1,0:T(8,128)(2,1)} %bitcast.290, ...), custom_call_target="tpu_custom_call" | custom-call | flops 4026531840 | bytes 12582912 | tf_op jit(solution)/shard_map/pallas_call | solution.py:83
  195.4 2.7 multiply_reduce_fusion.6
  206.4 4.5 all-to-all-start
  210.9 67.4 %all-gather.10.cloned.1.call-done = bf16[1,1,3072,768]{3,2,1,0:T(8,128)(2,1)} async-done(((bf16[1,1,768,768]{3,2,1,0:T(8,128)(2,1)}), bf16[1,1,3072,768]{3,2,1,0:T(8,128)(2,1)}) %all-gather.10.cloned.1.call-update) | async-done | bytes 4718608 | tf_op jit(solution)/shard_map/all_gather | solution.py:354
  278.4 54.1 %shard_map.197 = (bf16[1280,1536]{1,0:T(8,128)(2,1)}, f32[768,3072]{1,0:T(8,128)}, f32[768,3072]{1,0:T(8,128)}) custom-call(bf16[1280,1536]{1,0:T(8,128)(2,1)} %bitcast.24.xg_ref, bf16[768,3072]{1,0:T(8,128)(2,1)} %bitcast.285, bf16[3072,768]{1,0:T(8,128)(2,1)} %bitcast.287), custom_call_target="tpu_custom_call" | custom-call | flops 36238786560 | bytes 26738688 | tf_op jit(solution)/shard_map/pallas_call | solution.py:261
  332.5 4.9 all-to-all-start.1
  337.4 3.4 multiply_reduce_fusion.5
  340.9 42.8 %all-to-all-done.1 = bf16[8,160,1536]{2,1,0:T(8,128)(2,1)} async-done(((bf16[8,160,1536]{2,1,0:T(8,128)(2,1)}), bf16[8,160,1536]{2,1,0:T(8,128)(2,1)}, u32[]{:S(2)}, u32[]{:S(2)}) %all-to-all-start.1) | async-done | bytes 3932192 | tf_op jit(solution)/shard_map/all_to_all | solution.py:311
  383.7 3.7 fusion.3
  390.3 2.5 fusion.6
  392.8 3.2 multiply_reduce_fusion.2
  403.7 49.7 %all_to_all.20 = bf16[8,160,1536]{2,1,0:T(8,128)(2,1)} all-to-all(bf16[8,160,1536]{2,1,0:T(8,128)(2,1)S(1)} %bitcast.251), channel_id=1, replica_groups=mesh['dp'=8,'ctx'=4] {'dp'}, dimensions={0} | all-to-all | bytes 7864320 | tf_op jit(solution)/shard_map/all_to_all | solution.py:311
  453.3 55.1 %shard_map.198 = (bf16[1280,1536]{1,0:T(8,128)(2,1)}, bf16[768,3072]{1,0:T(8,128)(2,1)}, bf16[768,3072]{1,0:T(8,128)(2,1)}) custom-call(bf16[1280,1536]{1,0:T(8,128)(2,1)} %bitcast.258, bf16[768,3072]{1,0:T(8,128)(2,1)} %bitcast.286, bf16[3072,768]{1,0:T(8,128)(2,1)} %bitcast.288, f32[768,3072]{1,0:T(8,128)} %get-tuple-element.23.refs_0_, ...), custom_call_target="tpu_custom_call" | custom-call | flops 36238786560 | bytes 26738688 | tf_op jit(solution)/shard_map/pallas_call | solution.py:261
  508.4 4.6 all-to-all-start.3
  514.4 44.9 %all-to-all-done.3 = bf16[8,160,1536]{2,1,0:T(8,128)(2,1)} async-done(((bf16[8,160,1536]{2,1,0:T(8,128)(2,1)}), bf16[8,160,1536]{2,1,0:T(8,128)(2,1)}, u32[]{:S(2)}, u32[]{:S(2)}) %all-to-all-start.3) | async-done | bytes 3932192 | tf_op jit(solution)/shard_map/all_to_all | solution.py:311
  559.3 3.7 fusion.5
  565.9 2.5 fusion.10
  570.4 2.9 fusion.117
  581.8 3.6 copy.79
  588.4 93.9 %shard_map.199 = (bf16[2,512,768]{2,1,0:T(8,128)(2,1)}, bf16[2,1536,768]{2,1,0:T(8,128)(2,1)}, bf16[2,1536,768]{2,1,0:T(8,128)(2,1)}, f32[6,2,11,256]{3,2,1,0:T(8,128)}) custom-call(f32[6,2,1536]{2,1,0:T(2,128)} %reshape.436.line_ref, bf16[2,512,768]{2,1,0:T(8,128)(2,1)} %bitcast.298, bf16[2,1536,1536]{2,1,0:T(8,128)(2,1)} %bitcast.291, ...), custom_call_target="tpu_custom_call" | custom-call | flops 10066329600 | bytes 25165824 | tf_op jit(solution)/shard_map/pallas_call | solution.py:154
  682.3 7.9 bitcast_convert_fusion.1
  690.2 6.6 bitcast_convert_fusion
  696.8 2.9 bitcast_convert_fusion.2
  701.8 5.8 copy.92
  708.9 6.5 fusion.51
  715.5 5.3 convolution_add_fusion
  722.9 33.1 %collective-permute-done.2 = bf16[2,512,768]{2,1,0:T(8,128)(2,1)S(1)} collective-permute-done((bf16[2,512,768]{2,1,0:T(8,128)(2,1)S(1)}, bf16[2,512,768]{2,1,0:T(8,128)(2,1)S(1)}, u32[]{:S(2)}, u32[]{:S(2)}) %collective-permute-start.2) | collective-permute-done | bytes 1572896 | tf_op jit(solution)/shard_map/ppermute | solution.py:290
  760.9 4.3 fusion.53
  768.5 37.7 %collective-permute-done.3 = bf16[2,512,768]{2,1,0:T(8,128)(2,1)} collective-permute-done((bf16[2,512,768]{2,1,0:T(8,128)(2,1)}, bf16[2,512,768]{2,1,0:T(8,128)(2,1)}, u32[]{:S(2)}, u32[]{:S(2)}) %collective-permute-start.3) | collective-permute-done | bytes 1572896 | tf_op jit(solution)/shard_map/ppermute | solution.py:290
  806.2 6.3 fusion.19
  812.5 49.7 %all-reduce.3 = (f32[1,2,768]{2,1,0:T(2,128)}, f32[1,32,12]{1,2,0:T(8,128)S(1)}) all-reduce(f32[1,2,768]{2,1,0:T(2,128)S(1)} %maximum_bitcast_fusion, f32[1,32,12]{1,2,0:T(8,128)S(1)} %convolution_bitcast_fusion), channel_id=1, replica_groups=mesh['dp'=8,'ctx'=4] {'dp','ctx'}, use_global_device_ids=true, to_apply=%region_46.47 | all-reduce | flops 1920 | bytes 15360 | tf_op jit(solution)/shard_map/psum | solution.py:487
  862.8 3.7 fusion.15
  868.9 42.8 %reduce-scatter.9.cloned.1.call-done = bf16[768,768]{1,0:T(8,128)(2,1)} async-done(((bf16[768,3072]{1,0:T(8,128)(2,1)}), bf16[768,768]{1,0:T(8,128)(2,1)}) %reduce-scatter.9.cloned.1.call-update) | async-done | bytes 1179664 | tf_op jit(solution)/shard_map/reduce_scatter | solution.py:418
  911.7 2.8 convert_bitcast_fusion
  914.5 3.0 copy.88
  917.6 82.1 %reduce-scatter.7.cloned.1.call-done = bf16[768,768]{1,0:T(8,128)(2,1)} async-done(((bf16[768,3072]{1,0:T(8,128)(2,1)}), bf16[768,768]{1,0:T(8,128)(2,1)}) %reduce-scatter.7.cloned.1.call-update) | async-done | bytes 1179664 | tf_op jit(solution)/shard_map/reduce_scatter | solution.py:417
  999.6 2.8 bitcast_convert_fusion.3
  (259 shorter events, 76.2 us)
Async XLA Ops:
  7.2 129.7 %all-gather.6.cloned.1.call-start = ((), (), s32[]{:S(2)}) async-start(), calls=%async_computation.7 | async-start | bytes 5068800 | tf_op jit(solution)/shard_map/all_gather | solution.py:352
  9.8 3.7 copy-start
  10.5 200.4 %all-gather.8.cloned.1.call-start = ((), (), s32[]{:S(2)}) async-start(), calls=%async_computation.10 | async-start | bytes 5898240 | tf_op jit(solution)/shard_map/all_gather | solution.py:353
  13.4 8.0 copy-start.35
  13.4 8.4 copy-start.33
  13.4 8.5 copy-start.31
  13.4 14.4 %copy-start.36 = (f32[1,32,12]{1,0,2:T(1,128)S(1)}, f32[1,32,12]{1,0,2:T(1,128)}, u32[]{:S(2)}) copy-start(f32[1,32,12]{1,0,2:T(1,128)} %param.19) | copy-start | bytes 4612
  13.5 15.8 %copy-start.32 = (f32[1,2,768]{2,1,0:T(2,128)S(1)}, f32[1,2,768]{2,1,0:T(2,128)}, u32[]{:S(2)}) copy-start(f32[1,2,768]{2,1,0:T(2,128)} %param.18) | copy-start | bytes 18436
  13.5 264.9 %all-gather.10.cloned.1.call-start = ((), (), s32[]{:S(2)}) async-start(), calls=%async_computation.11 | async-start | bytes 5898240 | tf_op jit(solution)/shard_map/all_gather | solution.py:354
  13.5 51.6 %collective-permute-start = (bf16[2,512,768]{2,1,0:T(8,128)(2,1)S(1)}, bf16[2,512,768]{2,1,0:T(8,128)(2,1)S(1)}, u32[]{:S(2)}, u32[]{:S(2)}) collective-permute-start(bf16[2,512,768]{2,1,0:T(8,128)(2,1)S(1)} %copy-done), channel_id=1, source_target_pairs={{0,1},{1,2},{2,3},{4,5},{5,6},{6,7},{8,9},{9,10},{10,11},{12,13},{... | collective-permute-start | bytes 4718600 | tf_op jit(solution)/shard_map/ppermute | solution.py:290
  29.3 104.6 %copy-start.29 = (f32[768]{0:T(1024)}, f32[768]{0:T(1024)S(1)}, u32[]{:S(2)}) copy-start(f32[768]{0:T(1024)S(1)} %get-tuple-element.95) | copy-start | bytes 9220
  65.1 59.3 %collective-permute-start.1 = (bf16[2,512,768]{2,1,0:T(8,128)(2,1)S(1)}, bf16[2,512,768]{2,1,0:T(8,128)(2,1)S(1)}, u32[]{:S(2)}, u32[]{:S(2)}) collective-permute-start(bf16[2,512,768]{2,1,0:T(8,128)(2,1)S(1)} %collective-permute-done), channel_id=1, source_target_pairs={{0,1},{1,2},{2,3},{4,5},{5,6},{6,7},{8,9},{9,10},{10,11},{12,13},{... | collective-permute-start | bytes 4718600 | tf_op jit(solution)/shard_map/ppermute | solution.py:290
  129.0 2.1 copy-start.9
  133.9 3.0 copy-start.24
  136.9 4.0 copy-start.19
  195.4 3.0 copy-start.7
  195.4 3.0 copy-start.27
  198.3 2.6 copy-start.12
  200.7 3.1 copy-start.10
  206.4 72.0 %all-to-all-start = ((bf16[8,160,1536]{2,1,0:T(8,128)(2,1)}), bf16[8,160,1536]{2,1,0:T(8,128)(2,1)}, u32[]{:S(2)}, u32[]{:S(2)}) async-start(bf16[8,160,1536]{2,1,0:T(8,128)(2,1)} %bitcast.250), calls=%async_computation | async-start | bytes 7864320 | tf_op jit(solution)/shard_map/all_to_all | solution.py:311
  332.5 51.2 %all-to-all-start.1 = ((bf16[8,160,1536]{2,1,0:T(8,128)(2,1)}), bf16[8,160,1536]{2,1,0:T(8,128)(2,1)}, u32[]{:S(2)}, u32[]{:S(2)}) async-start(bf16[8,160,1536]{2,1,0:T(8,128)(2,1)} %bitcast.257), calls=%async_computation.1 | async-start | bytes 7864320 | tf_op jit(solution)/shard_map/all_to_all | solution.py:311
  390.3 2.5 copy-start.3
  392.8 3.3 copy-start.22
  392.8 4.8 copy-start.5
  392.8 4.8 copy-start.26
  396.0 3.9 copy-start.13
  400.0 3.1 copy-start.11
  508.4 50.9 %all-to-all-start.3 = ((bf16[8,160,1536]{2,1,0:T(8,128)(2,1)}), bf16[8,160,1536]{2,1,0:T(8,128)(2,1)}, u32[]{:S(2)}, u32[]{:S(2)}) async-start(bf16[8,160,1536]{2,1,0:T(8,128)(2,1)} %bitcast.256), calls=%async_computation.3 | async-start | bytes 7864320 | tf_op jit(solution)/shard_map/all_to_all | solution.py:311
  513.0 252.2 %all-reduce.6.cloned.1.call-start = ((), (), s32[]{:S(2)}) async-start(), calls=%async_computation.13 | async-start | bytes 2752512
  563.0 5.4 slice-start
  565.9 2.6 copy-start.4
  565.9 2.6 slice-start.1
  565.9 3.3 copy-start.23
  581.8 284.8 %reduce-scatter.11.cloned.1.call-start = ((), (), s32[]{:S(2)}) async-start(), calls=%async_computation.12 | async-start | bytes 3649536
  682.3 7.9 copy-start.37
  690.2 6.6 copy-start.38
  707.6 204.1 %reduce-scatter.9.cloned.1.call-start = ((), (), s32[]{:S(2)}) async-start(), calls=%async_computation.9 | async-start | bytes 5898240 | tf_op jit(solution)/shard_map/reduce_scatter | solution.py:418
  708.2 291.4 %reduce-scatter.7.cloned.1.call-start = ((), (), s32[]{:S(2)}) async-start(), calls=%async_computation.8 | async-start | bytes 5898240 | tf_op jit(solution)/shard_map/reduce_scatter | solution.py:417
  708.2 7.2 slice-start.2
  708.9 6.5 slice-start.3
  720.8 36.7 %copy-start.15 = (f32[3072,768]{1,0:T(8,128)}, f32[3072,768]{1,0:T(8,128)S(1)}, u32[]{:S(2)}) copy-start(f32[3072,768]{1,0:T(8,128)S(1)} %convolution_add_fusion) | copy-start | bytes 28311556
  720.9 35.0 %collective-permute-start.2 = (bf16[2,512,768]{2,1,0:T(8,128)(2,1)S(1)}, bf16[2,512,768]{2,1,0:T(8,128)(2,1)S(1)}, u32[]{:S(2)}, u32[]{:S(2)}) collective-permute-start(bf16[2,512,768]{2,1,0:T(8,128)(2,1)S(1)} %slice.412), channel_id=1, source_target_pairs={{1,0},{2,1},{3,2},{5,4},{6,5},{7,6},{9,8},{10,9},{11,10},{13,12},{... | collective-permute-start | bytes 4718600 | tf_op jit(solution)/shard_map/ppermute | solution.py:290
  722.8 36.1 %copy-start.28 = (f32[6,2,11,256]{3,2,1,0:T(8,128)S(1)}, f32[6,2,11,256]{3,2,1,0:T(8,128)}, u32[]{:S(2)}) copy-start(f32[6,2,11,256]{3,2,1,0:T(8,128)} %get-tuple-element.30) | copy-start | bytes 405508
  722.9 36.7 %copy-start.20 = (bf16[1,512,768]{2,1,0:T(8,128)(2,1)S(1)}, bf16[1,512,768]{2,1,0:T(8,128)(2,1)}, u32[]{:S(2)}) copy-start(bf16[1,512,768]{2,1,0:T(8,128)(2,1)} %get-tuple-element.109) | copy-start | bytes 2359300
  722.9 36.7 %copy-start.21 = (bf16[1,512,768]{2,1,0:T(8,128)(2,1)S(1)}, bf16[1,512,768]{2,1,0:T(8,128)(2,1)}, u32[]{:S(2)}) copy-start(bf16[1,512,768]{2,1,0:T(8,128)(2,1)} %get-tuple-element.110) | copy-start | bytes 2359300
  757.5 48.7 %collective-permute-start.3 = (bf16[2,512,768]{2,1,0:T(8,128)(2,1)}, bf16[2,512,768]{2,1,0:T(8,128)(2,1)}, u32[]{:S(2)}, u32[]{:S(2)}) collective-permute-start(bf16[2,512,768]{2,1,0:T(8,128)(2,1)} %fusion.21), channel_id=1, source_target_pairs={{1,0},{2,1},{3,2},{5,4},{6,5},{7,6},{9,8},{10,9},{11,10},{13,12},{... | collective-permute-start | bytes 4718600 | tf_op jit(solution)/shard_map/ppermute | solution.py:290
  760.9 45.3 %copy-start.30 = (f32[768]{0:T(1024)S(1)}, f32[768]{0:T(1024)}, u32[]{:S(2)}) copy-start(f32[768]{0:T(1024)} %copy-done.29) | copy-start | bytes 9220
  768.5 94.3 %copy-start.16 = (f32[1,512,768]{2,1,0:T(8,128)S(1)}, f32[1,512,768]{2,1,0:T(8,128)}, u32[]{:S(2)}) copy-start(f32[1,512,768]{2,1,0:T(8,128)} %get-tuple-element.100) | copy-start | bytes 4718596
  (10 other events, 16.5 us)
Sparse Core Ops, SparseCore 0:
  11.4 70.7 all-gather.5
  84.3 100.9 all-gather.7
  186.8 91.4 all-gather.9
  581.9 128.3 all-reduce.5
  715.5 108.5 reduce-scatter.10
  826.3 85.2 reduce-scatter.8
  914.0 85.6 reduce-scatter.6

commit v2 on v1

--- a/solution.py
+++ b/solution.py
@@ -7,6 +7,7 @@
 from jax.experimental.pallas import tpu as pltpu
 from jax.sharding import PartitionSpec as P
 
+
 HEADS=12; HEAD_DIM=64; NB=32; WIN=1024; TOP=2
 NEG=-1e30
 BUCKET_EDGES = [16, 21, 27, 35, 45, 58, 76, 98, 128, 166, 215, 279, 362, 470, 609, 790]
@@ -14,12 +15,16 @@
 
 NT=(((1,),(1,)),((),()))
 NN=(((1,),(0,)),((),()))
+
+
 def dot(a,b,dims): return lax.dot_general(a,b,dims,preferred_element_type=jnp.float32)
+
 
 def bucket_index(distance):
     edge_values = jnp.array(BUCKET_EDGES, dtype=jnp.int32)
     passed = jnp.sum((distance[..., None] >= edge_values).astype(jnp.int32), axis=-1)
     return jnp.where(distance < 16, distance, 15 + passed)
+
 
 def bias_line(table):
     n = GROWS + 128
@@ -28,6 +33,7 @@
     line = jnp.einsum("nb,bh->hn", hot, table, precision=lax.Precision.HIGHEST)
     line = jnp.where((d>=0)&(d<WIN), line, NEG)
     return line.reshape(HEADS//2,2,n)
+
 
 def spread_bias(line_ref, g_ref):
     for hh in range(2):
@@ -38,17 +44,22 @@
             x = pltpu.roll(x,0,1,stride=1,stride_axis=0)
             g_ref[hh, a*128:(a+1)*128,:] = x[:,128:256]
 
+
 def bias_chunk(g_ref, hh, r):
     o = pl.multiple_of(r*CB,CB) if not isinstance(r,int) else r*CB
     return jnp.concatenate([g_ref[hh, pl.ds(o+128,CB),:], g_ref[hh, pl.ds(o,CB),:]],axis=1)
 
+
 def rows8(x, op):
     return op(x.reshape(x.shape[0]//8,8,x.shape[1]),axis=0)
 
+
 def fwd_kernel(c0, line_ref, q_ref, k_ref, v_ref, qf_ref, kf_ref, o_ref, lse_ref, g_ref, kh_ref, qh_ref, vt_ref, s_ref, ot_ref):
     T=q_ref.shape[1]
+
     @pl.when(pl.program_id(1)==0)
     def _(): spread_bias(line_ref,g_ref)
+
     lane = lax.broadcasted_iota(jnp.int32,(1,128),1)
     vt_ref[...] = v_ref[0].T
     for hh in range(2):
@@ -78,17 +89,18 @@
             lse_ref[0,0,hh:hh+1,b*QB:(b+1)*QB]=m+jnp.log(l)
     o_ref[0]=ot_ref[...].T.astype(jnp.bfloat16)
 
-def attn_forward(line,q,kv,qf,kf,c0):
-    B,T,D=q.shape; K=kv.shape[1]; PR=D//128
+
+def attn_forward(line,q,kv,qf,kf,c0,m0,B):
+    _,T,D=q.shape; K=kv.shape[1]; PR=D//128
     return pl.pallas_call(
         partial(fwd_kernel,c0),
         grid=(PR,B),
         in_specs=[pl.BlockSpec((1,2,line.shape[2]),lambda p,m:(p,0,0)),
-                  pl.BlockSpec((1,T,128),lambda p,m:(m,0,p)),
-                  pl.BlockSpec((1,K,128),lambda p,m:(m,0,p)),
-                  pl.BlockSpec((1,K,128),lambda p,m:(m,0,PR+p)),
-                  pl.BlockSpec((1,T,128),lambda p,m:(m,0,0)),
-                  pl.BlockSpec((1,K,128),lambda p,m:(m,0,0))],
+                  pl.BlockSpec((1,T,128),lambda p,m:(m0+m,0,p)),
+                  pl.BlockSpec((1,K,128),lambda p,m:(m0+m,0,p)),
+                  pl.BlockSpec((1,K,128),lambda p,m:(m0+m,0,PR+p)),
+                  pl.BlockSpec((1,T,128),lambda p,m:(m0+m,0,0)),
+                  pl.BlockSpec((1,K,128),lambda p,m:(m0+m,0,0))],
         out_specs=[pl.BlockSpec((1,T,128),lambda p,m:(m,0,p)),
                    pl.BlockSpec((1,1,2,T),lambda p,m:(m,p,0,0))],
         out_shape=[jax.ShapeDtypeStruct((B,T,D),jnp.bfloat16),jax.ShapeDtypeStruct((B,PR,2,T),jnp.float32)],
@@ -97,14 +109,17 @@
         cost_estimate=pl.CostEstimate(flops=4*B*D*T*SPAN,bytes_accessed=2*B*D*(2*T+2*K),transcendentals=B*HEADS*T*SPAN),
     )(line,q,kv,kv,qf,kf)
 
+
 def bwd_kernel(c0, line_ref, q_ref, k_ref, v_ref, g_ref_in, qf_ref, kf_ref, lse_ref, dl_ref, dq_ref, dk_ref, dv_ref, tg_ref,
                g_ref, kh_ref, qh_ref, qz_ref, dz_ref, kt_ref, dk_acc, dv_acc, dqt_acc, t_acc):
     T=q_ref.shape[1]
     last=pl.num_programs(1)-1
+
     @pl.when(pl.program_id(1)==0)
     def _():
         spread_bias(line_ref,g_ref)
         t_acc[...]=jnp.zeros_like(t_acc)
+
     lane = lax.broadcasted_iota(jnp.int32,(1,128),1)
     kt_ref[...] = k_ref[0].T
     dk_acc[...]=jnp.zeros_like(dk_acc)
@@ -117,6 +132,7 @@
         dz_ref[hh] = jnp.where(mine,g_ref_in[0],jnp.zeros_like(q_ref[0]))
     dqt_acc[...]=jnp.zeros_like(dqt_acc)
     nb=T//QB
+
     def step(r,carry):
         for b in range(nb):
             for hh in range(2):
@@ -135,10 +151,12 @@
                 t_acc[hh,pl.ds(o+128,CB),:]+=ds[:,:128]
                 t_acc[hh,pl.ds(o,CB),:]+=ds[:,128:]
         return carry
+
     lax.fori_loop(0,SPAN//CB,step,0)
     dk_ref[0]=dk_acc[...].astype(jnp.bfloat16)
     dv_ref[0]=dv_acc[...].astype(jnp.bfloat16)
     dq_ref[0]=(dqt_acc[...].T*(HEAD_DIM**-0.5)).astype(jnp.bfloat16)
+
     @pl.when(pl.program_id(1)==last)
     def _():
         flip=(lax.broadcasted_iota(jnp.int32,(128,128),0)+lax.broadcasted_iota(jnp.int32,(128,128),1)==127).astype(jnp.float32)
@@ -149,18 +167,19 @@
                 x=pltpu.roll(x,0,1,stride=1,stride_axis=0)
                 tg_ref[0,hh,a:a+1,:]=jnp.sum(x,axis=0,keepdims=True)
 
-def attn_backward(line,q,kv,do,qf,kf,lse,dl,c0):
-    B,T,D=q.shape; K=kv.shape[1]; PR=D//128
+
+def attn_backward(line,q,kv,do,qf,kf,lse,dl,c0,m0):
+    T,D=q.shape[1:]; B=do.shape[0]; K=kv.shape[1]; PR=D//128
     return pl.pallas_call(
         partial(bwd_kernel,c0),
         grid=(PR,B),
         in_specs=[pl.BlockSpec((1,2,line.shape[2]),lambda p,m:(p,0,0)),
+                  pl.BlockSpec((1,T,128),lambda p,m:(m0+m,0,p)),
+                  pl.BlockSpec((1,K,128),lambda p,m:(m0+m,0,p)),
+                  pl.BlockSpec((1,K,128),lambda p,m:(m0+m,0,PR+p)),
                   pl.BlockSpec((1,T,128),lambda p,m:(m,0,p)),
-                  pl.BlockSpec((1,K,128),lambda p,m:(m,0,p)),
-                  pl.BlockSpec((1,K,128),lambda p,m:(m,0,PR+p)),
-                  pl.BlockSpec((1,T,128),lambda p,m:(m,0,p)),
-                  pl.BlockSpec((1,T,128),lambda p,m:(m,0,0)),
-                  pl.BlockSpec((1,K,128),lambda p,m:(m,0,0)),
+                  pl.BlockSpec((1,T,128),lambda p,m:(m0+m,0,0)),
+                  pl.BlockSpec((1,K,128),lambda p,m:(m0+m,0,0)),
                   pl.BlockSpec((1,1,2,T),lambda p,m:(m,p,0,0)),
                   pl.BlockSpec((1,1,2,T),lambda p,m:(m,p,0,0))],
         out_specs=[pl.BlockSpec((1,T,128),lambda p,m:(m,0,p)),
@@ -176,12 +195,14 @@
         cost_estimate=pl.CostEstimate(flops=10*B*D*T*SPAN,bytes_accessed=2*B*D*(2*T+2*K)*2,transcendentals=B*HEADS*T*SPAN),
     )(line,q,kv,kv,do,qf,kf,lse,dl)
 
+
 def table_from_diagonals(diag):
     d = WIN+128-128*jnp.arange(GSEG)[:,None]+(jnp.arange(256)[None,:]-127)
     hot=(jnp.clip(bucket_index(d),0,NB-1)[...,None]==jnp.arange(NB)).astype(jnp.float32)
     hot=hot*((d>=0)&(d<WIN)).astype(jnp.float32)[...,None]
     h=diag.reshape(HEADS,GSEG*256)
     return jnp.einsum("hn,nb->bh",h,hot.reshape(GSEG*256,NB),precision=lax.Precision.HIGHEST)
+
 
 def features(qdoc,kdoc,kvalid):
     lane=jnp.arange(128)%64
@@ -281,6 +302,141 @@
     )(xg, up, dn, *(prior if prior is not None else ()))
 
 
+MESH = pl.DeviceIdType.MESH
+
+
+def partners():
+    d, z = lax.axis_index("dp"), lax.axis_index("ctx")
+    core, x, y = d % 2, (d // 2) % 2, d // 4
+    return d, z, core, x, y, d + 1 - 2 * core, d + 2 - 4 * x, d + 4 - 8 * y
+
+
+def greet(peers):
+    barrier = pltpu.get_barrier_semaphore()
+    for peer in peers:
+        pl.semaphore_signal(barrier, inc=1, device_id=peer, device_id_type=MESH)
+    pl.semaphore_wait(barrier, len(peers))
+
+
+def sum_kernel(widths, split, Z, *refs):
+    n = len(widths)
+    parts, small, outs, small_out = refs[:n], refs[n], refs[n + 1 : 2 * n + 1], refs[2 * n + 1]
+    got1 = refs[2 * n + 2 : 3 * n + 2]
+    keep1 = refs[3 * n + 2 : 4 * n + 2]
+    got2 = refs[4 * n + 2 : 5 * n + 2]
+    keep2 = refs[5 * n + 2 : 6 * n + 2]
+    got3 = refs[6 * n + 2 : 7 * n + 2]
+    keep3 = refs[7 * n + 2 : 8 * n + 2]
+    got4 = refs[8 * n + 2 : 9 * n + 2]
+    s_keep, s_got, send, recv = refs[9 * n + 2 :]
+    d, z, core, x, y, pc, px, py = partners()
+    zs = [(z + k) % Z for k in range(1, Z)]
+    peers = [(pc, z), (px, z), (py, z)] + [(d, t) for t in zs]
+    greet(peers)
+    low, wide = jnp.bfloat16, jnp.float32
+
+    def push(src, dst, i, peer):
+        copy = pltpu.make_async_remote_copy(
+            src_ref=src,
+            dst_ref=dst,
+            send_sem=send.at[i],
+            recv_sem=recv.at[i],
+            device_id=peer,
+            device_id_type=MESH,
+        )
+        copy.start()
+        return copy
+
+    s_keep[0] = small[...]
+
+    stage = [push(parts[j].at[:, :, 1 - core], got1[j], j, (pc, z)) for j in range(n)]
+    tiny = push(s_keep.at[0], s_got.at[0], 4 * n, (pc, z))
+    order = list(range(n))
+    stage2 = [None] * n
+    for j in order:
+        stage[j].wait()
+        first = j < split
+        for a in range(2):
+            for b in range(2):
+                if first:
+                    keep1[j][b, a] = (parts[j][a, b, core].astype(wide) + got1[j][a, b].astype(wide)).astype(low)
+                else:
+                    keep1[j][a, b] = (parts[j][a, b, core].astype(wide) + got1[j][a, b].astype(wide)).astype(low)
+        mine, peer = (x, (px, z)) if first else (y, (py, z))
+        stage2[j] = push(keep1[j].at[1 - mine], got2[j], n + j, peer)
+    tiny.wait()
+    s_keep[1] = s_keep[0] + s_got[0]
+    tiny = push(s_keep.at[1], s_got.at[1], 4 * n + 1, (px, z))
+    stage3 = [None] * n
+    for j in order:
+        stage2[j].wait()
+        first = j < split
+        mine, then, peer = (x, y, (py, z)) if first else (y, x, (px, z))
+        for a in range(2):
+            keep2[j][a] = (keep1[j][mine, a].astype(wide) + got2[j][a].astype(wide)).astype(low)
+        stage3[j] = push(keep2[j].at[1 - then], got3[j], 2 * n + j, peer)
+    tiny.wait()
+    s_keep[2] = s_keep[1] + s_got[1]
+    tiny = push(s_keep.at[2], s_got.at[2], 4 * n + 2, (py, z))
+    stage4 = []
+    base = 4 * n + 3
+    for j in order:
+        stage3[j].wait()
+        then = y if j < split else x
+        keep3[j][...] = (keep2[j][then].astype(wide) + got3[j][...].astype(wide)).astype(low)
+        for k in range(Z - 1):
+            stage4.append(push(keep3[j].at[zs[k]], got4[j].at[k], base + j * (Z - 1) + k, (d, zs[k])))
+    tiny.wait()
+    s_keep[3] = s_keep[2] + s_got[2]
+    base = base + n * (Z - 1)
+    tinies = [push(s_keep.at[3], s_got.at[3 + z], base + k, (d, zs[k])) for k in range(Z - 1)]
+    for copy in stage4:
+        copy.wait()
+    for j in order:
+        total = keep3[j][z].astype(wide)
+        for k in range(Z - 1):
+            total = total + got4[j][k].astype(wide)
+        outs[j][...] = total
+    for copy in tinies:
+        copy.wait()
+    total = None
+    for t in range(Z):
+        term = jnp.where(z == t, s_keep[3], s_got[3 + t])
+        total = term if total is None else total + term
+    small_out[...] = total
+
+
+def sum_over_all(parts, split, small):
+    Z = lax.axis_size("ctx")
+    rows = parts[0].shape[0] // (8 * Z)
+    widths = [p.shape[1] for p in parts]
+    n = len(parts)
+    views = [p.astype(jnp.bfloat16).reshape(2, 2, 2, Z, rows, w) for p, w in zip(parts, widths)]
+    vm = pl.BlockSpec(memory_space=pltpu.VMEM)
+    low = jnp.bfloat16
+
+    def buf(*lead):
+        return [pltpu.VMEM(lead + (rows, w), low) for w in widths]
+
+    sems = 4 * n + 3 + n * (Z - 1) + (Z - 1)
+    out = pl.pallas_call(
+        partial(sum_kernel, widths, split, Z),
+        in_specs=[vm] * (n + 1),
+        out_specs=[vm] * (n + 1),
+        out_shape=[jax.ShapeDtypeStruct((rows, w), jnp.float32) for w in widths]
+        + [jax.ShapeDtypeStruct(small.shape, jnp.float32)],
+        scratch_shapes=buf(2, 2, Z) + buf(2, 2, Z) + buf(2, Z) + buf(2, Z) + buf(Z) + buf(Z) + buf(Z - 1)
+        + [
+            pltpu.VMEM((4,) + small.shape, jnp.float32),
+            pltpu.VMEM((3 + Z,) + small.shape, jnp.float32),
+            pltpu.SemaphoreType.DMA((sems,)),
+            pltpu.SemaphoreType.DMA((sems,)),
+        ],
+        compiler_params=pltpu.CompilerParams(collective_id=1, has_side_effects=True),
+    )(*views, small)
+    return out[:n], out[n]
+
+
 EPS = 1e-06
 
 
@@ -315,7 +471,7 @@
     return jnp.dot(a, b, preferred_element_type=jnp.float32)
 
 
-def on_device(
+def layer(
     tokens,
     cotangent,
     proj_weights,
@@ -370,12 +526,18 @@
     normed_own = normed[:, K - T :]
     q = (mm(normed_own.reshape(B * T, D), w_q).astype(low) * low(HEAD_DIM**-0.5)).reshape(B, T, D)
 
-    attn, lse = attn_forward(line, q, kv, qf, kf, c0)
-
     expert_ids = jnp.arange(experts, dtype=jnp.int32)
     slot_range = jnp.arange(slots, dtype=jnp.int32)
     kept = []
+    attns = []
+    lses = []
     for m in range(B):
+        attn, lse = attn_forward(line, q, kv, qf, kf, c0, m, 1)
+        attn = attn[0]
+        if kept:
+            attn, _ = lax.optimization_barrier((attn, kept[-1][-2]))
+        attns.append(attn)
+        lses.append(lse)
         route_now = routes[m]
         picks = (route_now[:, :, None] == expert_ids).astype(jnp.float32)
         order_hot = (jnp.transpose(route_now).reshape(-1)[:, None] == expert_ids[None, :]).astype(
@@ -390,7 +552,7 @@
 
         resid = tokens[m].astype(jnp.float32)
         d_out = cotangent[m]
-        middle = resid + mm(attn[m], w_out)
+        middle = resid + mm(attns[m], w_out)
         two_low = rms_norm(middle, gains[1]).astype(low)
         logits = mm(two_low, w_router)
         gates = gate_values(logits, picks)
@@ -404,28 +566,37 @@
             [sent[:, :D].astype(low), (sent[:, D:] * slot_gate[:, None]).astype(low)], axis=1
         )
         received = exchange(payload, ranks)
-        kept.append((picks, hot, table, middle, two_low, logits, slot_gate, d_rows, received))
+        kept.append((picks, hot, table, middle, two_low, logits, slot_gate, d_rows, payload, received))
 
     prior = None
     returned = []
     for m in range(B):
         last = m == B - 1
-        back, up_part, dn_part = expert_step(kept[m][-1], up_full, dn_full, prior, last)
+        received = kept[m][-1]
+        back, up_part, dn_part = expert_step(received, up_full, dn_full, prior, last)
         prior = (up_part, dn_part)
+        if not last:
+            back, ahead = lax.optimization_barrier((back, kept[m + 1][-1]))
+            kept[m + 1] = kept[m + 1][:-1] + (ahead,)
         returned.append(exchange(back, ranks))
     up_part, dn_part = prior
     up_grad = lax.psum_scatter(up_part, "ctx", scatter_dimension=1, tiled=True)
     dn_grad = lax.psum_scatter(dn_part, "ctx", scatter_dimension=1, tiled=True)
 
     outputs = []
-    mids = []
-    d_branches = []
-    d_attns = []
     router_grad = 0.0
+    out_grad = 0.0
+    gain_one = 0.0
     gain_two = 0.0
+    table_grad = 0.0
+    tokens_grads = []
+    q_grad = k_grad = v_grad = 0.0
+    chains = []
     for m in range(B):
-        picks, hot, table, middle, two_low, logits, slot_gate, d_rows, _ = kept[m]
+        picks, hot, table, middle, two_low, logits, slot_gate, d_rows, _, _ = kept[m]
         back = returned[m]
+        if chains:
+            back, _ = lax.optimization_barrier((back, delta))
         d_resid = cotangent[m].astype(jnp.float32)
         slot_dgate = jnp.sum(d_rows.astype(jnp.float32) * back[:, :D].astype(jnp.float32), axis=1)
         d_gates = jnp.stack(
@@ -445,57 +616,66 @@
         gain_two = gain_two + gain_part
         d_mid = d_resid + d_norm
         d_branch = d_mid.astype(low)
-        mids.append(d_mid)
-        d_branches.append(d_branch)
-        d_attns.append(mm(d_branch, w_out.T).astype(low))
-    d_attn = jnp.stack(d_attns)
-    d_branch = jnp.concatenate(d_branches)
-    out_grad = mm(attn.reshape(B * T, D).T, d_branch)
-    delta = jnp.sum(
-        (attn.astype(jnp.float32) * d_attn.astype(jnp.float32)).reshape(B, T, HEADS, HEAD_DIM), axis=-1
-    )
-    delta = jnp.transpose(delta, (0, 2, 1)).reshape(B, HEADS // 2, 2, T)
-    dq, dk, dv, diag = attn_backward(line, q, kv, d_attn, qf, kf, lse, delta, c0)
-    table_grad = table_from_diagonals(diag)
-
-    d_normed = (mm(dk.reshape(B * K, D), w_k.T) + mm(dv.reshape(B * K, D), w_v.T)).reshape(B, K, D)
-    carried = d_normed[:, :T]
-    for hop in range(hops - 1, -1, -1):
-        start = (hops - hop) * T
-        carried = (
-            passed_along(carried.astype(low), "ctx", -1).astype(jnp.float32)
-            + d_normed[:, start : start + T]
-        )
-    own = carried + mm(dq.reshape(B * T, D), w_q.T).reshape(B, T, D)
-    normed_rows = normed.reshape(B * K, D)
-    proj_grad = jnp.concatenate(
-        [
-            mm(normed_own.reshape(B * T, D).T, dq.reshape(B * T, D)),
-            mm(normed_rows.T, dk.reshape(B * K, D)),
-            mm(normed_rows.T, dv.reshape(B * K, D)),
-        ],
-        axis=1,
-    ).astype(low)
-    d_first, gain_one = jax.vjp(rms_norm, tokens.astype(jnp.float32), gains[0])[1](own)
-    tokens_grad = (jnp.stack(mids) + d_first).astype(low)
-
-    side = jnp.concatenate(
-        [out_grad, jnp.pad(router_grad, ((0, 0), (0, 128 - experts)))], axis=1
-    ).astype(low)
-    side_part = lax.psum_scatter(side, ("dp", "ctx"), scatter_dimension=0, tiled=True)
-    proj_part = lax.psum_scatter(proj_grad, ("dp", "ctx"), scatter_dimension=0, tiled=True)
-    gains_total, table_total = lax.psum(
-        (jnp.stack([gain_one, gain_two])[None], table_grad[None]), ("dp", "ctx")
-    )
+        d_attn = mm(d_branch, w_out.T).astype(low)
+        out_grad = out_grad + mm(attns[m].T, d_branch)
+        delta = jnp.sum(
+            (attns[m].astype(jnp.float32) * d_attn.astype(jnp.float32)).reshape(T, HEADS, HEAD_DIM),
+            axis=-1,
+        )
+        delta = delta.T.reshape(1, HEADS // 2, 2, T)
+        dq, dk, dv, diag = attn_backward(
+            line, q, kv, d_attn[None], qf, kf, lses[m], delta, c0, m
+        )
+        dq, dk, dv = dq[0], dk[0], dv[0]
+        table_grad = table_grad + table_from_diagonals(diag)
+        far = K - T
+        d_far = mm(dk[:far], w_k.T) + mm(dv[:far], w_v.T)
+        carried = d_far[:T]
+        for hop in range(hops - 1, 0, -1):
+            start = (hops - hop) * T
+            carried = passed_along(carried.astype(low), "ctx", -1)
+            carried = carried.astype(jnp.float32) + d_far[start : start + T]
+        carried = passed_along(carried.astype(low), "ctx", -1)
+        own = mm(dk[far:], w_k.T) + mm(dv[far:], w_v.T) + mm(dq, w_q.T)
+        chains.append((carried, own, d_mid))
+        q_grad = q_grad + mm(normed[m, far:].T, dq)
+        k_grad = k_grad + mm(normed[m].T, dk)
+        v_grad = v_grad + mm(normed[m].T, dv)
+    for m in range(B):
+        carried, own, d_mid = chains[m]
+        d_first, gain_part = jax.vjp(rms_norm, tokens[m].astype(jnp.float32), gains[0])[1](
+            own + carried.astype(jnp.float32)
+        )
+        gain_one = gain_one + gain_part
+        tokens_grads.append((d_mid + d_first).astype(low))
+
+    router_wide = jnp.pad(router_grad, ((0, 0), (0, 128 - experts)))
+    small = jnp.concatenate([gain_one, gain_two, table_grad.reshape(-1)])
+    if ranks == 8 and D % (16 * lax.axis_size("ctx")) == 0:
+        small = jnp.pad(small, (0, 2048 - small.shape[0])).reshape(8, 256)
+        parts, small = sum_over_all([q_grad, k_grad, router_wide, v_grad, out_grad], 3, small)
+        small = small.reshape(-1)
+        proj_part = jnp.concatenate([parts[0], parts[1], parts[3]], axis=1)
+        router_part, out_part = parts[2], parts[4]
+    else:
+        joined = jnp.concatenate([q_grad, k_grad, v_grad, out_grad, router_wide], axis=1).astype(low)
+        joined = lax.psum_scatter(joined, ("dp", "ctx"), scatter_dimension=0, tiled=True)
+        joined = joined.astype(jnp.float32)
+        small = lax.psum(small, ("dp", "ctx"))
+        proj_part, out_part, router_part = (
+            joined[:, : 3 * D],
+            joined[:, 3 * D : 4 * D],
+            joined[:, 4 * D :],
+        )
     wide = jnp.float32
     return (
         jnp.stack(outputs),
-        tokens_grad,
-        proj_part.astype(wide)[None],
-        side_part[:, :D].astype(wide)[None],
-        side_part[:, D : D + experts].astype(wide)[None],
-        gains_total,
-        table_total,
+        jnp.stack(tokens_grads),
+        proj_part[None],
+        out_part[None],
+        router_part[None, :, :experts],
+        small[: 2 * D].reshape(1, 2, D),
+        small[2 * D : 2 * D + NB * HEADS].reshape(1, NB, HEADS),
         up_grad.astype(wide)[None, None],
         dn_grad.astype(wide).T[None, None],
     )
@@ -526,6 +706,4 @@
         P(None, "dp", None, "ctx"),
         P(None, "dp", "ctx", None),
     )
-    return jax.shard_map(
-        on_device, mesh=mesh, in_specs=in_specs, out_specs=out_specs, check_vma=False
-    )
+    return jax.shard_map(layer, mesh=mesh, in_specs=in_specs, out_specs=out_specs, check_vma=False)

time: 1010 us -> 793 us (0.79)
  waiting for transfers between devices: 432 us -> 221 us
  blocking collectives: 99.4 us -> 0 us
  Pallas kernels: 246 us -> 305 us
  matrix products: 76.9 us -> 92 us
    reduce_scatter x2, waiting for transfers between devices: 125 us -> 0.01 us  [the longest x1 0.01 us: layer(): dn_grad = lax.psum_scatter(dn_part, 'ctx', scatter_dimension=1, tiled=True)]
    all_gather x3, waiting for transfers between devices: 67.5 us -> 9.3 us  [the longest x1 9.29 us: layer(): lax.all_gather(down_weights[0, 0].astype(low), 'ctx', axis=0, tiled=True)]
    psum x1 -> x0, blocking collectives: 49.7 us -> none  [on_device(): lax.psum((jnp.stack([gain_one, gain_two])[None], table_grad[None]), ('dp'...]
    all_to_all x1 -> x0, blocking collectives: 49.7 us -> none  [exchange(): lax.all_to_all(blocks, 'dp', split_axis=0, concat_axis=0, tiled=True)]
    pallas_call x0 -> x1, Pallas kernels: none -> 45.7 us  [sum_over_all(): pl.pallas_call(partial(sum_kernel, widths, split, Z), in_specs=[vm] * (n...]
    ppermute x4 -> x6, waiting for transfers between devices: 151 us -> 109 us  [passed_along(): return lax.ppermute(block, axis, route)]
    all_to_all x3 -> x4, waiting for transfers between devices: 87.7 us -> 102 us  [exchange(): lax.all_to_all(blocks, 'dp', split_axis=0, concat_axis=0, tiled=True)]
    dot_general x21 -> x32, matrix products: 70.9 us -> 85.5 us  [mm(): return jnp.dot(a, b, preferred_element_type=jnp.float32)]
  transfers between devices with their start and end apart: 14 -> 15, of which waited for: 9 -> 8; matrix products, arithmetic and copies ran while one was open for 13% -> 24% of each run, Pallas kernels for 14% -> 32%
where the time goes in v2:
time: 793 us; the launch traced here: 789 us
  Pallas kernels  305 us (38%)
  waiting for transfers between devices  221 us (28%)
  matrix products  92 us (12%)
  other arithmetic  78.2 us (10%)
  local copies, waits for them, and re-layouts  41.7 us (5%)
  starting transfers between devices  36.1 us (5%)
  between operations  15.6 us (2%)
    pallas_call x2, Pallas kernels, expert_step(): pl.pallas_call(partial(expert_kernel, prior is not None), grid=(F // FC,)...  109 us
    ppermute x6, waiting for transfers between devices, passed_along(): return lax.ppermute(block, axis, route)  109 us
    pallas_call x2, Pallas kernels, attn_backward(): pl.pallas_call(partial(bwd_kernel, c0), grid=(PR, B), in_specs=[pl.BlockS...  108 us
    all_to_all x4, waiting for transfers between devices, exchange(): lax.all_to_all(blocks, 'dp', split_axis=0, concat_axis=0, tiled=True)  102 us
    dot_general x32, matrix products, mm(): return jnp.dot(a, b, preferred_element_type=jnp.float32)  85.5 us
    pallas_call x1, Pallas kernels, sum_over_all(): pl.pallas_call(partial(sum_kernel, widths, split, Z), in_specs=[vm] * (n...  45.7 us
    pallas_call x2, Pallas kernels, attn_forward(): pl.pallas_call(partial(fwd_kernel, c0), grid=(PR, B), in_specs=[pl.BlockS...  41.5 us
    unnamed x137, local copies, waits for them, and re-layouts  19.2 us
  transfers between devices with their start and end apart: 15, of which 8 were waited for; matrix products, arithmetic and copies ran while one was open for 24% of the time, Pallas kernels for 32%

profile of v2, /device:TPU:0, one launch (start us, length us, event | category | flops | bytes accessed | tf_op | source)
XLA Modules:
  0.0 788.9 jit_solution(14647037063098240593)
XLA Ops:
  10.6 2.9 convert_element_type.242
  13.7 5.1 collective-permute-start
  18.7 2.8 convert_element_type.244
  32.9 32.5 %collective-permute-done = bf16[2,512,768]{2,1,0:T(8,128)(2,1)S(1)} collective-permute-done((bf16[2,512,768]{2,1,0:T(8,128)(2,1)S(1)}, bf16[2,512,768]{2,1,0:T(8,128)(2,1)S(1)}, u32[]{:S(2)}, u32[]{:S(2)}) %collective-permute-start) | collective-permute-done | bytes 1572896 | tf_op jit(solution)/shard_map/ppermute | solution.py:446
  65.4 6.8 collective-permute-start.1
  74.4 3.2 iota_compare_fusion
  77.5 47.9 %collective-permute-done.1 = bf16[2,512,768]{2,1,0:T(8,128)(2,1)S(1)} collective-permute-done((bf16[2,512,768]{2,1,0:T(8,128)(2,1)S(1)}, bf16[2,512,768]{2,1,0:T(8,128)(2,1)S(1)}, u32[]{:S(2)}, u32[]{:S(2)}) %collective-permute-start.1) | collective-permute-done | bytes 1572896 | tf_op jit(solution)/shard_map/ppermute | solution.py:446
  133.8 3.0 fusion.1
  136.8 4.0 fusion.60
  140.8 11.2 %convolution_convert_fusion = bf16[3072,1536]{1,0:T(8,128)(2,1)} fusion(bf16[3072,768]{1,0:T(8,128)(2,1)S(1)} %copy-done.26, bf16[768,3200]{1,0:T(8,128)(2,1)} %all-gather.6.cloned.1.call-done), kind=kOutput, calls=%fused_computation | convolution fusion | flops 7252475904 | bytes 16515072 | tf_op jit(solution)/shard_map/dot_general | solution.py:471
  152.0 20.8 %shard_map.205 = (bf16[1,512,768]{2,1,0:T(8,128)(2,1)}, f32[1,6,2,512]{3,2,1,0:T(2,128)}) custom-call(f32[6,2,1536]{2,1,0:T(2,128)} %reshape.510.line_ref, bf16[2,512,768]{2,1,0:T(8,128)(2,1)} %bitcast.301, bf16[2,1536,1536]{2,1,0:T(8,128)(2,1)} %bitcast.291, bf16[2,1536,1536]{2,1,0:T(8,128)(2,1)} %bitcast.292, ...), custom_call_target="tpu_custom_call" | custom-call | flops 2013265920 | bytes 6291456 | tf_op jit(solution)/shard_map/pallas_call | solution.py:95
  179.9 3.2 copy-done.16
  186.0 20.7 %shard_map.207 = (bf16[1,512,768]{2,1,0:T(8,128)(2,1)}, f32[1,6,2,512]{3,2,1,0:T(2,128)}) custom-call(f32[6,2,1536]{2,1,0:T(2,128)} %reshape.510.line_ref, bf16[2,512,768]{2,1,0:T(8,128)(2,1)} %bitcast.302, bf16[2,1536,1536]{2,1,0:T(8,128)(2,1)} %bitcast.293, bf16[2,1536,1536]{2,1,0:T(8,128)(2,1)} %bitcast.294, ...), custom_call_target="tpu_custom_call" | custom-call | flops 2013265920 | bytes 6291456 | tf_op jit(solution)/shard_map/pallas_call | solution.py:95
  213.8 4.5 all-to-all-start
  230.7 33.9 %all-to-all-done = bf16[8,160,1536]{2,1,0:T(8,128)(2,1)} async-done(((bf16[8,160,1536]{2,1,0:T(8,128)(2,1)}), bf16[8,160,1536]{2,1,0:T(8,128)(2,1)}, u32[]{:S(2)}, u32[]{:S(2)}) %all-to-all-start) | async-done | bytes 3932192 | tf_op jit(solution)/shard_map/all_to_all | solution.py:467
  264.6 4.5 all-to-all-start.1
  269.2 9.3 %all-gather.10.cloned.1.call-done = bf16[1,1,3072,768]{3,2,1,0:T(8,128)(2,1)} async-done(((bf16[1,1,768,768]{3,2,1,0:T(8,128)(2,1)}), bf16[1,1,3072,768]{3,2,1,0:T(8,128)(2,1)}) %all-gather.10.cloned.1.call-update) | async-done | bytes 4718608 | tf_op jit(solution)/shard_map/all_gather | solution.py:510
  278.5 54.2 %shard_map.206 = (bf16[1280,1536]{1,0:T(8,128)(2,1)}, f32[768,3072]{1,0:T(8,128)}, f32[768,3072]{1,0:T(8,128)}) custom-call(bf16[1280,1536]{1,0:T(8,128)(2,1)} %bitcast.24.xg_ref, bf16[768,3072]{1,0:T(8,128)(2,1)} %bitcast.352, bf16[3072,768]{1,0:T(8,128)(2,1)} %bitcast.354), custom_call_target="tpu_custom_call" | custom-call | flops 36238786560 | bytes 26738688 | tf_op jit(solution)/shard_map/pallas_call | solution.py:282
  332.7 55.0 %shard_map.208 = (bf16[1280,1536]{1,0:T(8,128)(2,1)}, bf16[768,3072]{1,0:T(8,128)(2,1)}, bf16[768,3072]{1,0:T(8,128)(2,1)}) custom-call(bf16[1280,1536]{1,0:T(8,128)(2,1)} %bitcast.39.xg_ref, bf16[768,3072]{1,0:T(8,128)(2,1)} %bitcast.353, bf16[3072,768]{1,0:T(8,128)(2,1)} %bitcast.355, f32[768,3072]{1,0:T(8,128)} %get-tuple-element.43.refs_0_, ...), custom_call_target="tpu_custom_call" | custom-call | flops 36238786560 | bytes 26738688 | tf_op jit(solution)/shard_map/pallas_call | solution.py:282
  387.8 4.5 all-to-all-start.2
  393.1 45.5 %all-to-all-done.2 = bf16[8,160,1536]{2,1,0:T(8,128)(2,1)} async-done(((bf16[8,160,1536]{2,1,0:T(8,128)(2,1)}), bf16[8,160,1536]{2,1,0:T(8,128)(2,1)}, u32[]{:S(2)}, u32[]{:S(2)}) %all-to-all-start.2) | async-done | bytes 3932192 | tf_op jit(solution)/shard_map/all_to_all | solution.py:467
  438.6 4.5 all-to-all-start.3
  445.4 3.8 fusion.3
  454.7 2.9 fusion.73
  457.6 3.5 convert_multiply_fusion.13
  461.1 3.0 copy.54
  466.4 23.1 %all-to-all-done.3 = bf16[8,160,1536]{2,1,0:T(8,128)(2,1)} async-done(((bf16[8,160,1536]{2,1,0:T(8,128)(2,1)}), bf16[8,160,1536]{2,1,0:T(8,128)(2,1)}, u32[]{:S(2)}, u32[]{:S(2)}) %all-to-all-start.3) | async-done | bytes 3932192 | tf_op jit(solution)/shard_map/all_to_all | solution.py:467
  489.4 4.6 fusion.5
  502.9 4.1 convert_multiply_fusion.12
  507.0 3.0 copy.55
  512.3 54.2 %shard_map.210 = (bf16[1,512,768]{2,1,0:T(8,128)(2,1)}, bf16[1,1536,768]{2,1,0:T(8,128)(2,1)}, bf16[1,1536,768]{2,1,0:T(8,128)(2,1)}, f32[6,2,11,256]{3,2,1,0:T(8,128)}) custom-call(f32[6,2,1536]{2,1,0:T(2,128)} %reshape.510.line_ref, bf16[2,512,768]{2,1,0:T(8,128)(2,1)} %bitcast.303, bf16[2,1536,1536]{2,1,0:T(8,128)(2,1)} %bitcast.295, ...), custom_call_target="tpu_custom_call" | custom-call | flops 5033164800 | bytes 12582912 | tf_op jit(solution)/shard_map/pallas_call | solution.py:173
  566.4 3.3 fusion.51
  576.4 54.1 %shard_map.209 = (bf16[1,512,768]{2,1,0:T(8,128)(2,1)}, bf16[1,1536,768]{2,1,0:T(8,128)(2,1)}, bf16[1,1536,768]{2,1,0:T(8,128)(2,1)}, f32[6,2,11,256]{3,2,1,0:T(8,128)}) custom-call(f32[6,2,1536]{2,1,0:T(2,128)} %reshape.510.line_ref, bf16[2,512,768]{2,1,0:T(8,128)(2,1)} %bitcast.304, bf16[2,1536,1536]{2,1,0:T(8,128)(2,1)} %bitcast.297, ...), custom_call_target="tpu_custom_call" | custom-call | flops 5033164800 | bytes 12582912 | tf_op jit(solution)/shard_map/pallas_call | solution.py:173
  630.5 3.3 fusion.54
  633.9 2.8 convolution_add_fusion.1
  638.7 3.4 fusion.80
  646.5 3.3 fusion.88
  661.5 3.2 add_convert_fusion.1
  664.9 3.8 fusion.19
  678.9 5.7 add_convert_fusion.2
  684.6 15.2 %collective-permute-done.5 = bf16[512,768]{1,0:T(8,128)(2,1)} collective-permute-done((bf16[512,768]{1,0:T(8,128)(2,1)}, bf16[512,768]{1,0:T(8,128)(2,1)}, u32[]{:S(2)}, u32[]{:S(2)}) %collective-permute-start.5) | collective-permute-done | bytes 786464 | tf_op jit(solution)/shard_map/ppermute | solution.py:446
  699.8 13.0 %collective-permute-done.3 = bf16[512,768]{1,0:T(8,128)(2,1)} collective-permute-done((bf16[512,768]{1,0:T(8,128)(2,1)}, bf16[512,768]{1,0:T(8,128)(2,1)}, u32[]{:S(2)}, u32[]{:S(2)}) %collective-permute-start.3) | collective-permute-done | bytes 786464 | tf_op jit(solution)/shard_map/ppermute | solution.py:446
  712.8 4.0 fusion.33
  717.4 45.7 %shard_map.211 = (f32[24,768]{1,0:T(8,128)}, f32[24,768]{1,0:T(8,128)}, f32[24,128]{1,0:T(8,128)}, f32[24,768]{1,0:T(8,128)}, f32[24,768]{1,0:T(8,128)}, /*index=5*/f32[8,256]{1,0:T(8,128)}) custom-call(bf16[2,2,2,4,24,768]{5,4,3,2,1,0:T(8,128)(2,1)} %bitcast.311, bf16[2,2,2,4,24,768]{5,4,3,2,1,0:T(8,128)(2,1)} %bitcast.322, ...), custom_call_target="tpu_custom_call" | custom-call | tf_op jit(solution)/shard_map/pallas_call | solution.py:422
  767.3 3.2 fusion.76
  772.5 2.8 convert_bitcast_fusion
  775.4 3.0 copy.60
  778.4 2.9 bitcast_convert_fusion
  (320 shorter events, 118.5 us)
Async XLA Ops:
  7.2 129.6 %all-gather.6.cloned.1.call-start = ((), (), s32[]{:S(2)}) async-start(), calls=%async_computation.6 | async-start | bytes 5068800 | tf_op jit(solution)/shard_map/all_gather | solution.py:508
  10.6 258.6 %all-gather.8.cloned.1.call-start = ((), (), s32[]{:S(2)}) async-start(), calls=%async_computation.9 | async-start | bytes 5898240 | tf_op jit(solution)/shard_map/all_gather | solution.py:509
  13.6 8.0 %copy-start.56 = (s32[2,4]{1,0:T(2,128)S(1)}, s32[2,4]{1,0:T(2,128)}, u32[]{:S(2)}) copy-start(s32[2,4]{1,0:T(2,128)} %param.23) | copy-start | bytes 100
  13.6 8.4 %copy-start.55 = (s32[16]{0:T(128)S(1)}, s32[16]{0:T(128)}, u32[]{:S(2)}) copy-start(s32[16]{0:T(128)} %constant.108.clone) | copy-start | bytes 196
  13.6 8.5 %copy-start.53 = (s32[2,512,2]{1,2,0:T(2,128)S(1)}, s32[2,512,2]{1,2,0:T(2,128)}, u32[]{:S(2)}) copy-start(s32[2,512,2]{1,2,0:T(2,128)} %param.24) | copy-start | bytes 24580
  13.6 14.3 %copy-start.57 = (f32[1,32,12]{1,0,2:T(1,128)S(1)}, f32[1,32,12]{1,0,2:T(1,128)}, u32[]{:S(2)}) copy-start(f32[1,32,12]{1,0,2:T(1,128)} %param.20) | copy-start | bytes 4612
  13.6 264.9 %all-gather.10.cloned.1.call-start = ((), (), s32[]{:S(2)}) async-start(), calls=%async_computation.10 | async-start | bytes 5898240 | tf_op jit(solution)/shard_map/all_gather | solution.py:510
  13.7 51.8 %collective-permute-start = (bf16[2,512,768]{2,1,0:T(8,128)(2,1)S(1)}, bf16[2,512,768]{2,1,0:T(8,128)(2,1)S(1)}, u32[]{:S(2)}, u32[]{:S(2)}) collective-permute-start(bf16[2,512,768]{2,1,0:T(8,128)(2,1)S(1)} %copy-done), channel_id=1, source_target_pairs={{0,1},{1,2},{2,3},{4,5},{5,6},{6,7},{8,9},{9,10},{10,11},{12,13},{... | collective-permute-start | bytes 4718600 | tf_op jit(solution)/shard_map/ppermute | solution.py:446
  21.5 7.8 copy-start.54
  29.4 104.4 %copy-start.47 = (f32[768]{0:T(1024)}, f32[768]{0:T(1024)S(1)}, u32[]{:S(2)}) copy-start(f32[768]{0:T(1024)S(1)} %get-tuple-element.124) | copy-start | bytes 9220
  65.4 59.9 %collective-permute-start.1 = (bf16[2,512,768]{2,1,0:T(8,128)(2,1)S(1)}, bf16[2,512,768]{2,1,0:T(8,128)(2,1)S(1)}, u32[]{:S(2)}, u32[]{:S(2)}) collective-permute-start(bf16[2,512,768]{2,1,0:T(8,128)(2,1)S(1)} %collective-permute-done), channel_id=1, source_target_pairs={{0,1},{1,2},{2,3},{4,5},{5,6},{6,7},{8,9},{9,10},{10,11},{12,13},{... | collective-permute-start | bytes 4718600 | tf_op jit(solution)/shard_map/ppermute | solution.py:446
  136.8 4.0 copy-start.26
  175.2 277.7 %copy-start.8 = (f32[512,768]{1,0:T(8,128)}, f32[512,768]{1,0:T(8,128)S(1)}, u32[]{:S(2)}) copy-start(f32[512,768]{1,0:T(8,128)S(1)} %get-tuple-element.154) | copy-start | bytes 4718596
  175.4 9.2 %copy-start.20 = (bf16[512,768]{1,0:T(8,128)(2,1)}, bf16[512,768]{1,0:T(8,128)(2,1)S(1)}, u32[]{:S(2)}) copy-start(bf16[512,768]{1,0:T(8,128)(2,1)S(1)} %multiply_convert_fusion.4) | copy-start | bytes 2359300
  179.9 3.2 copy-start.16
  213.8 50.8 %all-to-all-start = ((bf16[8,160,1536]{2,1,0:T(8,128)(2,1)}), bf16[8,160,1536]{2,1,0:T(8,128)(2,1)}, u32[]{:S(2)}, u32[]{:S(2)}) async-start(bf16[8,160,1536]{2,1,0:T(8,128)(2,1)} %bitcast.305), calls=%async_computation | async-start | bytes 7864320 | tf_op jit(solution)/shard_map/all_to_all | solution.py:467
  222.1 3.3 copy-start.18
  264.6 68.1 %all-to-all-start.1 = ((bf16[8,160,1536]{2,1,0:T(8,128)(2,1)}), bf16[8,160,1536]{2,1,0:T(8,128)(2,1)}, u32[]{:S(2)}, u32[]{:S(2)}) async-start(bf16[8,160,1536]{2,1,0:T(8,128)(2,1)} %bitcast.306), calls=%async_computation.1 | async-start | bytes 7864320 | tf_op jit(solution)/shard_map/all_to_all | solution.py:467
  269.1 503.4 %reduce-scatter.5.cloned.1.call-start = ((), (), s32[]{:S(2)}) async-start(), calls=%async_computation.8 | async-start | bytes 5898240 | tf_op jit(solution)/shard_map/reduce_scatter | solution.py:584
  387.8 50.8 %all-to-all-start.2 = ((bf16[8,160,1536]{2,1,0:T(8,128)(2,1)}), bf16[8,160,1536]{2,1,0:T(8,128)(2,1)}, u32[]{:S(2)}, u32[]{:S(2)}) async-start(bf16[8,160,1536]{2,1,0:T(8,128)(2,1)} %bitcast.314), calls=%async_computation.2 | async-start | bytes 7864320 | tf_op jit(solution)/shard_map/all_to_all | solution.py:467
  438.6 50.8 %all-to-all-start.3 = ((bf16[8,160,1536]{2,1,0:T(8,128)(2,1)}), bf16[8,160,1536]{2,1,0:T(8,128)(2,1)}, u32[]{:S(2)}, u32[]{:S(2)}) async-start(bf16[8,160,1536]{2,1,0:T(8,128)(2,1)} %bitcast.313), calls=%async_computation.3 | async-start | bytes 7864320 | tf_op jit(solution)/shard_map/all_to_all | solution.py:467
  443.1 335.3 %reduce-scatter.3.cloned.1.call-start = ((), (), s32[]{:S(2)}) async-start(), calls=%async_computation.7 | async-start | bytes 5898240 | tf_op jit(solution)/shard_map/reduce_scatter | solution.py:583
  445.4 3.9 copy-start.12
  502.9 4.1 copy-start.2
  566.4 3.3 copy-start.22
  575.1 93.6 %collective-permute-start.4 = (bf16[512,768]{1,0:T(8,128)(2,1)}, bf16[512,768]{1,0:T(8,128)(2,1)}, u32[]{:S(2)}, u32[]{:S(2)}) collective-permute-start(bf16[512,768]{1,0:T(8,128)(2,1)} %slice.553), channel_id=1, source_target_pairs={{1,0},{2,1},{3,2},{5,4},{6,5},{7,6},{9,8},{10,9},{11,10},{13,12},{... | collective-permute-start | bytes 2359304 | tf_op jit(solution)/shard_map/ppermute | solution.py:446
  630.5 3.4 copy-start.40
  630.5 12.0 %slice-start.2 = ((s8[4915200]{0:T(1024)(128)(4,1)}), s8[4194304]{0:T(1024)(128)(4,1)S(1)}, s32[]{:S(2)}) async-start(s8[4915200]{0:T(1024)(128)(4,1)} %bitcast.309), calls=%async_computation.13 | async-start | bytes 8388608
  633.8 4.6 copy-start.45
  633.8 4.7 copy-start.46
  633.8 8.7 %slice-start.3 = ((s8[4915200]{0:T(1024)(128)(4,1)}), s8[720896]{0:T(1024)(128)(4,1)S(1)}, s32[]{:S(2)}) async-start(s8[4915200]{0:T(1024)(128)(4,1)} %bitcast.309), calls=%async_computation.14 | async-start | bytes 1441792
  636.7 35.5 %collective-permute-start.2 = (bf16[512,768]{1,0:T(8,128)(2,1)S(1)}, bf16[512,768]{1,0:T(8,128)(2,1)S(1)}, u32[]{:S(2)}, u32[]{:S(2)}) collective-permute-start(bf16[512,768]{1,0:T(8,128)(2,1)S(1)} %slice.554), channel_id=1, source_target_pairs={{1,0},{2,1},{3,2},{5,4},{6,5},{7,6},{9,8},{10,9},{11,10},{13,12},{... | collective-permute-start | bytes 2359304 | tf_op jit(solution)/shard_map/ppermute | solution.py:446
  638.7 3.8 copy-start.31
  644.5 9.2 %slice-start = ((s8[4718592]{0:T(1024)(128)(4,1)}), s8[4194304]{0:T(1024)(128)(4,1)S(1)}, s32[]{:S(2)}) async-start(s8[4718592]{0:T(1024)(128)(4,1)} %bitcast.299), calls=%async_computation.11 | async-start | bytes 8388608
  646.5 3.3 copy-start.44
  646.5 7.2 slice-start.1
  661.5 3.2 copy-start.19
  664.9 3.8 copy-start.14
  671.0 28.8 %collective-permute-start.5 = (bf16[512,768]{1,0:T(8,128)(2,1)}, bf16[512,768]{1,0:T(8,128)(2,1)}, u32[]{:S(2)}, u32[]{:S(2)}) collective-permute-start(bf16[512,768]{1,0:T(8,128)(2,1)} %fusion.38), channel_id=1, source_target_pairs={{1,0},{2,1},{3,2},{5,4},{6,5},{7,6},{9,8},{10,9},{11,10},{13,12},{... | collective-permute-start | bytes 2359304 | tf_op jit(solution)/shard_map/ppermute | solution.py:446
  673.3 39.5 %collective-permute-start.3 = (bf16[512,768]{1,0:T(8,128)(2,1)}, bf16[512,768]{1,0:T(8,128)(2,1)}, u32[]{:S(2)}, u32[]{:S(2)}) collective-permute-start(bf16[512,768]{1,0:T(8,128)(2,1)} %fusion.39), channel_id=1, source_target_pairs={{1,0},{2,1},{3,2},{5,4},{6,5},{7,6},{9,8},{10,9},{11,10},{13,12},{... | collective-permute-start | bytes 2359304 | tf_op jit(solution)/shard_map/ppermute | solution.py:446
  675.4 3.4 copy-start.32
  678.9 33.9 %copy-start.33 = (f32[512,768]{1,0:T(8,128)S(1)}, f32[512,768]{1,0:T(8,128)}, u32[]{:S(2)}) copy-start(f32[512,768]{1,0:T(8,128)} %fusion.80) | copy-start | bytes 4718596
  678.9 33.9 %copy-start.34 = (f32[512,768]{1,0:T(8,128)S(1)}, f32[512,768]{1,0:T(8,128)}, u32[]{:S(2)}) copy-start(f32[512,768]{1,0:T(8,128)} %fusion.82) | copy-start | bytes 4718596
  678.9 33.9 %copy-start.35 = (f32[512,768]{1,0:T(8,128)S(1)}, f32[512,768]{1,0:T(8,128)}, u32[]{:S(2)}) copy-start(f32[512,768]{1,0:T(8,128)} %fusion.86) | copy-start | bytes 4718596
  678.9 33.9 %copy-start.36 = (f32[512,768]{1,0:T(8,128)S(1)}, f32[512,768]{1,0:T(8,128)}, u32[]{:S(2)}) copy-start(f32[512,768]{1,0:T(8,128)} %fusion.88) | copy-start | bytes 4718596
  678.9 33.9 %copy-start.37 = (f32[512,768]{1,0:T(8,128)S(1)}, f32[512,768]{1,0:T(8,128)}, u32[]{:S(2)}) copy-start(f32[512,768]{1,0:T(8,128)} %fusion.68) | copy-start | bytes 4718596
  678.9 33.9 %copy-start.38 = (f32[512,768]{1,0:T(8,128)S(1)}, f32[512,768]{1,0:T(8,128)}, u32[]{:S(2)}) copy-start(f32[512,768]{1,0:T(8,128)} %fusion.70) | copy-start | bytes 4718596
  678.9 33.9 %copy-start.48 = (f32[768]{0:T(1024)S(1)}, f32[768]{0:T(1024)}, u32[]{:S(2)}) copy-start(f32[768]{0:T(1024)} %copy-done.47) | copy-start | bytes 9220
  (29 other events, 58.8 us)
Sparse Core Ops, SparseCore 0:
  11.4 70.5 all-gather.5
  83.6 101.7 all-gather.7
  187.0 91.4 all-gather.9
  387.9 93.8 reduce-scatter.4
  483.9 85.7 reduce-scatter.2
